TPU v7x, 32 devices: a 4x4x1 block of a 4x4x8 slice. The times are simulated.
32 devices in a mesh: rep: 2 (over z, core), dp: 16 (over x, y).
Axes of the slice: x: 4, y: 4, z: 1, core: 2. Of those that a mesh axis runs over, the one named last changes fastest.
The devices are a block of a 4x4x8 slice.
Arguments:
- x: bfloat16 [32, 4096, 512], P(('rep', 'dp')), parts along dimension 0
- dy: bfloat16 [32, 4096, 512], P(('rep', 'dp')), parts along dimension 0
- w_gate: bfloat16 [2, 512, 1408], P(None, 'dp')
- w_up: bfloat16 [2, 512, 1408], P(None, 'dp')
- w_down: bfloat16 [2, 1408, 512], P(None, 'dp')
- m_w_gate: float32 [2, 512, 1408], P(None, 'dp')
- m_w_up: float32 [2, 512, 1408], P(None, 'dp')
- m_w_down: float32 [2, 1408, 512], P(None, 'dp')
- v_w_gate: float32 [2, 512, 1408], P(None, 'dp')
- v_w_up: float32 [2, 512, 1408], P(None, 'dp')
- v_w_down: float32 [2, 1408, 512], P(None, 'dp')
Outputs:
- output 1: bfloat16 [4, 512, 1408], P('rep', 'dp'), parts along dimension 0
- output 2: bfloat16 [4, 512, 1408], P('rep', 'dp'), parts along dimension 0
- output 3: bfloat16 [4, 1408, 512], P('rep', 'dp'), parts along dimension 0
- output 4: float32 [4, 512, 1408], P('rep', 'dp'), parts along dimension 0
- output 5: float32 [4, 512, 1408], P('rep', 'dp'), parts along dimension 0
- output 6: float32 [4, 1408, 512], P('rep', 'dp'), parts along dimension 0
- output 7: float32 [4, 512, 1408], P('rep', 'dp'), parts along dimension 0
- output 8: float32 [4, 512, 1408], P('rep', 'dp'), parts along dimension 0
- output 9: float32 [4, 1408, 512], P('rep', 'dp'), parts along dimension 0
There are 2 independent parts. A program takes and returns all parts, laid end to end along the dimension named above; an argument that names none is the same for every part.
All inputs are finite; a program needn't handle non-finite values.
Results may differ from a plain program's by a relative error of at most 0.022.
Values are sent between devices in bfloat16 or wider.
A program may use at most 768 MiB of HBM per device.

v0:
```python
import jax
import jax.numpy as jnp
from jax import lax
from jax.sharding import PartitionSpec as P

NAMES = ("w_gate", "w_up", "w_down")


def matmul(a, w):
    return jnp.dot(a, w, preferred_element_type=jnp.float32).astype(jnp.bfloat16)


def normed(h):
    wide = h.astype(jnp.float32)
    scale = lax.rsqrt(jnp.mean(wide**2, -1, keepdims=True) + 1e-6)
    return (wide * scale).astype(jnp.bfloat16)


def layer(h, w):
    a = normed(h)
    gate = jnp.dot(a, w["w_gate"], preferred_element_type=jnp.float32)
    up = jnp.dot(a, w["w_up"], preferred_element_type=jnp.float32)
    return h + matmul((jax.nn.silu(gate) * up).astype(jnp.bfloat16), w["w_down"])


def adamw(w, m, v, g):
    m = 0.9 * m + 0.1 * g
    v = 0.95 * v + 0.05 * g * g
    step = m * lax.rsqrt(v + 1e-8) + 0.1 * w
    return (w - 0.02 * step).astype(jnp.bfloat16), m, v


def clipped(gradients, sum_of_squares, count):
    factor = jnp.minimum(1.0, 0.5 * lax.rsqrt(sum_of_squares / count + 1e-30))
    return [g * factor for g in gradients]


def solution(mesh):
    def fetched(weights, number):
        return {name: lax.all_gather(w[number], "dp", axis=0, tiled=True) for name, w in zip(NAMES, weights, strict=True)}

    def step(x, dy, *arrays):
        weights, m, v = (arrays[i : i + 3] for i in (0, 3, 6))
        layers = weights[0].shape[0]
        h, kept = x[0], []
        for number in range(layers):
            kept.append(h)
            h = layer(h, fetched(weights, number))
        by_h, mine = dy[0], [None] * layers
        for number in reversed(range(layers)):
            _, back = jax.vjp(lambda w, h: layer(h, w), fetched(weights, number), kept[number])
            by_w, by_h = back(by_h)
            mine[number] = [lax.psum_scatter(by_w[name], "dp", scatter_dimension=0, tiled=True) for name in NAMES]
        gradients = [jnp.stack([mine[number][i] for number in range(layers)]).astype(jnp.float32) for i in range(3)]
        squares = lax.psum(sum(jnp.sum(g * g) for g in gradients), "dp")
        gradients = clipped(gradients, squares, lax.psum(1, "dp") * sum(g.size for g in gradients))
        new = [adamw(w.astype(jnp.float32), m, v, g) for w, m, v, g in zip(weights, m, v, gradients, strict=True)]
        return tuple(one[which] for which in range(3) for one in new)

    states, cut = P(("rep", "dp"), None, None), P(None, "dp", None)
    return jax.shard_map(
        step,
        mesh=mesh,
        in_specs=(states, states) + (cut,) * 9,
        out_specs=(P("rep", "dp", None),) * 9,
        check_vma=False,
    )
```

profile of v0, /device:TPU:96, one launch (start us, length us, event | category | flops | bytes accessed | tf_op | source)
XLA Modules:
  0.0 786.1 jit_solution(3363062136134420337)
XLA Ops:
  30.2 21.2 %all-gather.13.cloned.1.call-done = bf16[1,512,1408]{2,1,0:T(8,128)(2,1)} async-done(((bf16[1,32,1408]{2,1,0:T(8,128)(2,1)}), bf16[1,512,1408]{2,1,0:T(8,128)(2,1)}) %all-gather.13.cloned.1.call-update) | async-done | bytes 1441808 | tf_op jit(solution)/shard_map/all_gather | solution.py:40
  51.4 13.2 %fusion.47 = f32[4096,1408]{1,0:T(8,128)} fusion(bf16[1,4096,512]{1,2,0:T(8,128)(2,1)} %copy.22, f32[4096]{0:T(1024)S(1)} %add_rsqrt_fusion, bf16[1,512,1408]{2,1,0:T(8,128)(2,1)} %all-gather.13.cloned.1.call-done), kind=kOutput, calls=%fused_computation.57 | convolution fusion | flops 5911871488 | bytes 28721152 | tf_op jit(solution)/shard_map/dot_general | solution.py:21
  64.6 27.0 %all-gather.15.cloned.1.call-done = bf16[1,512,1408]{2,1,0:T(8,128)(2,1)} async-done(((bf16[1,32,1408]{2,1,0:T(8,128)(2,1)}), bf16[1,512,1408]{2,1,0:T(8,128)(2,1)}) %all-gather.15.cloned.1.call-update) | async-done | bytes 1441808 | tf_op jit(solution)/shard_map/all_gather | solution.py:40
  91.6 24.3 %multiply_convert_fusion.1 = (bf16[4096,1408]{1,0:T(8,128)(2,1)}, f32[4096,1408]{1,0:T(8,128)}) fusion(f32[4096,1408]{1,0:T(8,128)} %fusion.47, bf16[1,512,1408]{2,1,0:T(8,128)(2,1)} %all-gather.15.cloned.1.call-done, bf16[1,4096,512]{1,2,0:T(8,128)(2,1)} %copy.22, f32[4096]{0:T(1024)S(1)} %add_rsqrt_fusion), kind=kOutput, calls=%fused_computation.17 | convolution fusion | flops 5946474496 | bytes 63324160 | tf_op jit(solution)/shard_map/dot_general | solution.py:22
  115.9 15.8 %all-gather.17.cloned.1.call-done = bf16[1,1408,512]{2,1,0:T(8,128)(2,1)} async-done(((bf16[1,88,512]{2,1,0:T(8,128)(2,1)}), bf16[1,1408,512]{2,1,0:T(8,128)(2,1)}) %all-gather.17.cloned.1.call-update) | async-done | bytes 1441808 | tf_op jit(solution)/shard_map/all_gather | solution.py:40
  131.7 12.4 %fusion.19 = (f32[4096]{0:T(1024)S(1)}, bf16[4096,512]{0,1:T(8,128)(2,1)}) fusion(bf16[4096,1408]{1,0:T(8,128)(2,1)} %get-tuple-element.24, bf16[1,1408,512]{2,1,0:T(8,128)(2,1)} %all-gather.17.cloned.1.call-done, bf16[1,4096,512]{1,2,0:T(8,128)(2,1)} %copy.22), kind=kOutput, calls=%fused_computation.37 | convolution fusion | flops 5916061696 | bytes 21381120 | tf_op jit(solution)/shard_map/dot_general | solution.py:10
  144.8 27.0 %all-gather.21.cloned.1.call-done = bf16[1,1408,512]{2,1,0:T(8,128)(2,1)} async-done(((bf16[1,88,512]{2,1,0:T(8,128)(2,1)}), bf16[1,1408,512]{2,1,0:T(8,128)(2,1)}) %all-gather.21.cloned.1.call-update) | async-done | bytes 1441808 | tf_op jit(solution)/shard_map/all_gather | solution.py:40
  171.8 11.8 %convolution_convert_fusion.1 = bf16[4096,1408]{1,0:T(8,128)(2,1)} fusion(bf16[1,4096,512]{2,1,0:T(8,128)(2,1)} %param.12, bf16[1,1408,512]{2,1,0:T(8,128)(2,1)} %all-gather.21.cloned.1.call-done), kind=kOutput, calls=%fused_computation.23 | convolution fusion | flops 5911347200 | bytes 17170432 | tf_op jit(solution)/shard_map/transpose(jvp())/dot_general | solution.py:10
  183.5 28.2 %all-gather.23.cloned.1.call-done = bf16[1,512,1408]{2,1,0:T(8,128)(2,1)} async-done(((bf16[1,32,1408]{2,1,0:T(8,128)(2,1)}), bf16[1,512,1408]{2,1,0:T(8,128)(2,1)}) %all-gather.23.cloned.1.call-update) | async-done | bytes 1441808 | tf_op jit(solution)/shard_map/all_gather | solution.py:40
  211.8 13.1 %fusion.39 = f32[4096,1408]{1,0:T(8,128)} fusion(bf16[4096,512]{0,1:T(8,128)(2,1)} %get-tuple-element.27, f32[4096]{0:T(1024)S(1)} %fusion.79, bf16[1,512,1408]{2,1,0:T(8,128)(2,1)} %all-gather.23.cloned.1.call-done), kind=kOutput, calls=%fused_computation.54 | convolution fusion | flops 5911871488 | bytes 28721152 | tf_op jit(solution)/shard_map/jvp()/dot_general | solution.py:22
  224.9 26.9 %all-gather.19.cloned.1.call-done = bf16[1,512,1408]{2,1,0:T(8,128)(2,1)} async-done(((bf16[1,32,1408]{2,1,0:T(8,128)(2,1)}), bf16[1,512,1408]{2,1,0:T(8,128)(2,1)}) %all-gather.19.cloned.1.call-update) | async-done | bytes 1441808 | tf_op jit(solution)/shard_map/all_gather | solution.py:40
  251.8 31.8 %fusion.2 = (bf16[4096,1408]{1,0:T(8,128)(2,1)}, f32[4096,1408]{1,0:T(8,128)}) fusion(f32[4096,1408]{1,0:T(8,128)} %fusion.39, bf16[4096,1408]{1,0:T(8,128)(2,1)} %convolution_convert_fusion.1, bf16[1,512,1408]{2,1,0:T(8,128)(2,1)} %all-gather.19.cloned.1.call-done, bf16[4096,512]{0,1:T(8,128)(2,1)} %get-tuple-element.27, f32[4096]{0:T(1024)S(1)} %fusion.79), kind=kOutput, calls=%fused_computation.8 | convolution fusion | flops 5981077504 | bytes 74858496 | tf_op jit(solution)/shard_map/jvp()/dot_general | solution.py:21
  283.6 22.3 %convolution_convert_fusion.5 = bf16[512,1408]{1,0:T(8,128)(2,1)} fusion(bf16[4096,1408]{1,0:T(8,128)(2,1)} %get-tuple-element.28, bf16[4096,512]{0,1:T(8,128)(2,1)} %get-tuple-element.27, f32[4096]{0:T(1024)S(1)} %fusion.79), kind=kOutput, calls=%fused_computation.53 | convolution fusion | flops 5911871488 | bytes 17186816 | tf_op jit(solution)/shard_map/transpose(jvp())/dot_general | solution.py:21
  306.1 17.2 %fusion.22 = bf16[4096,512]{0,1:T(8,128)(2,1)} fusion(bf16[4096,1408]{1,0:T(8,128)(2,1)} %convolution_convert_fusion.1, bf16[1,512,1408]{2,1,0:T(8,128)(2,1)} %all-gather.23.cloned.1.call-done, f32[4096,1408]{1,0:T(8,128)} %get-tuple-element.29), kind=kOutput, calls=%fused_computation.40 | convolution fusion | flops 5942280192 | bytes 40239104 | tf_op jit(solution)/shard_map/transpose(jvp())/dot_general | solution.py:22
  346.9 24.6 %fusion.33 = bf16[512,1408]{1,0:T(8,128)(2,1)} fusion(f32[4096,1408]{1,0:T(8,128)} %fusion.47, f32[4096,1408]{1,0:T(8,128)} %get-tuple-element.25, bf16[4096,1408]{1,0:T(8,128)(2,1)} %convolution_convert_fusion, bf16[1,4096,512]{1,2,0:T(8,128)(2,1)} %copy.22, f32[4096]{0:T(1024)S(1)} %copy-done.15), kind=kOutput, calls=%fused_computation.50 | convolution fusion | flops 5976031232 | bytes 63324160 | tf_op jit(solution)/shard_map/transpose(jvp())/dot_general | solution.py:21
  371.6 17.2 %fusion.32 = bf16[512,1408]{1,0:T(8,128)(2,1)} fusion(bf16[4096,1408]{1,0:T(8,128)(2,1)} %convolution_convert_fusion.1, bf16[4096,512]{0,1:T(8,128)(2,1)} %get-tuple-element.27, f32[4096]{0:T(1024)S(1)} %fusion.79, f32[4096,1408]{1,0:T(8,128)} %get-tuple-element.29), kind=kOutput, calls=%fused_computation.49 | convolution fusion | flops 5947195392 | bytes 40255488 | tf_op jit(solution)/shard_map/transpose(jvp())/dot_general | solution.py:22
  389.0 17.6 %fusion.36 = bf16[512,1408]{1,0:T(8,128)(2,1)} fusion(bf16[4096,1408]{1,0:T(8,128)(2,1)} %convolution_convert_fusion, f32[4096,1408]{1,0:T(8,128)} %fusion.47, bf16[1,4096,512]{1,2,0:T(8,128)(2,1)} %copy.22, f32[4096]{0:T(1024)S(1)} %copy-done.15), kind=kOutput, calls=%fused_computation.51 | convolution fusion | flops 5947195392 | bytes 40255488 | tf_op jit(solution)/shard_map/transpose(jvp())/dot_general | solution.py:22
  406.7 20.4 %fusion.29 = bf16[1408,512]{1,0:T(8,128)(2,1)} fusion(bf16[1,4096,512]{2,1,0:T(8,128)(2,1)} %param.12, f32[4096,1408]{1,0:T(8,128)} %fusion.39, f32[4096,1408]{1,0:T(8,128)} %get-tuple-element.29), kind=kOutput, calls=%fused_computation.48 | convolution fusion | flops 5940903936 | bytes 51773440 | tf_op jit(solution)/shard_map/transpose(jvp())/dot_general | solution.py:10
  427.4 12.4 %convolution_convert_fusion.4 = bf16[1408,512]{1,0:T(8,128)(2,1)} fusion(bf16[4096,1408]{1,0:T(8,128)(2,1)} %get-tuple-element.24, bf16[4096,512]{0,1:T(8,128)(2,1)} %copy-done.2), kind=kOutput, calls=%fused_computation.52 | convolution fusion | flops 5906300928 | bytes 17170432 | tf_op jit(solution)/shard_map/transpose(jvp())/dot_general | solution.py:10
  448.2 70.1 %reduce-scatter.17.cloned.1.call-done = bf16[32,1408]{1,0:T(8,128)(2,1)} async-done(((bf16[512,1408]{1,0:T(8,128)(2,1)}), bf16[32,1408]{1,0:T(8,128)(2,1)}) %reduce-scatter.17.cloned.1.call-update) | async-done | bytes 90128 | tf_op jit(solution)/shard_map/reduce_scatter | solution.py:53
  518.3 71.5 %reduce-scatter.15.cloned.1.call-done = bf16[32,1408]{1,0:T(8,128)(2,1)} async-done(((bf16[512,1408]{1,0:T(8,128)(2,1)}), bf16[32,1408]{1,0:T(8,128)(2,1)}) %reduce-scatter.15.cloned.1.call-update) | async-done | bytes 90128 | tf_op jit(solution)/shard_map/reduce_scatter | solution.py:53
  592.7 68.8 %reduce-scatter.21.cloned.1.call-done = bf16[88,512]{1,0:T(8,128)(2,1)} async-done(((bf16[1408,512]{1,0:T(8,128)(2,1)}), bf16[88,512]{1,0:T(8,128)(2,1)}) %reduce-scatter.21.cloned.1.call-update) | async-done | bytes 90128
  661.5 71.5 %reduce-scatter.19.cloned.1.call-done = bf16[88,512]{1,0:T(8,128)(2,1)} async-done(((bf16[1408,512]{1,0:T(8,128)(2,1)}), bf16[88,512]{1,0:T(8,128)(2,1)}) %reduce-scatter.19.cloned.1.call-update) | async-done | bytes 90128
  735.3 38.7 %psum.7 = f32[]{:T(128)} all-reduce(f32[]{:T(128)S(6)} %add.99), channel_id=1, replica_groups=mesh['rep'=2,'dp'=16] {'dp'}, use_global_device_ids=true, to_apply=%region_12.13 | all-reduce | flops 1 | bytes 8 | tf_op jit(solution)/shard_map/psum | solution.py:55
  (77 shorter events, 63.8 us)
Async XLA Ops:
  7.2 44.2 %all-gather.13.cloned.1.call-start = ((), (), s32[]{:S(2)}) async-start(), calls=%async_computation.10 | async-start | bytes 1531904 | tf_op jit(solution)/shard_map/all_gather | solution.py:40
  8.9 82.6 %all-gather.15.cloned.1.call-start = ((), (), s32[]{:S(2)}) async-start(), calls=%async_computation.11 | async-start | bytes 1531904 | tf_op jit(solution)/shard_map/all_gather | solution.py:40
  10.7 121.0 %all-gather.17.cloned.1.call-start = ((), (), s32[]{:S(2)}) async-start(), calls=%async_computation.12 | async-start | bytes 1531904 | tf_op jit(solution)/shard_map/all_gather | solution.py:40
  12.4 159.3 %all-gather.21.cloned.1.call-start = ((), (), s32[]{:S(2)}) async-start(), calls=%async_computation.14 | async-start | bytes 1531904 | tf_op jit(solution)/shard_map/all_gather | solution.py:40
  13.1 198.7 %all-gather.23.cloned.1.call-start = ((), (), s32[]{:S(2)}) async-start(), calls=%async_computation.15 | async-start | bytes 1531904 | tf_op jit(solution)/shard_map/all_gather | solution.py:40
  13.7 238.1 %all-gather.19.cloned.1.call-start = ((), (), s32[]{:S(2)}) async-start(), calls=%async_computation.13 | async-start | bytes 1531904 | tf_op jit(solution)/shard_map/all_gather | solution.py:40
  14.4 425.5 %reduce-scatter.13.cloned.1.call-start = ((), (), s32[]{:S(2)}) async-start(), calls=%async_computation.7 | async-start | bytes 1531904 | tf_op jit(solution)/shard_map/reduce_scatter | solution.py:53
  23.9 67.7 %copy-start.14 = (f32[4096]{0:T(1024)}, f32[4096]{0:T(1024)S(1)}, u32[]{:S(2)}) copy-start(f32[4096]{0:T(1024)S(1)} %add_rsqrt_fusion) | copy-start | bytes 49156
  306.0 140.5 %reduce-scatter.11.cloned.1.call-start = ((), (), s32[]{:S(2)}) async-start(), calls=%async_computation.6 | async-start | bytes 1531904 | tf_op jit(solution)/shard_map/reduce_scatter | solution.py:53
  306.1 17.2 %copy-start.1 = (bf16[4096,512]{0,1:T(8,128)(2,1)S(1)}, bf16[4096,512]{0,1:T(8,128)(2,1)}, u32[]{:S(2)}) copy-start(bf16[4096,512]{0,1:T(8,128)(2,1)} %get-tuple-element.27) | copy-start | bytes 12582916
  323.2 11.2 %copy-start = (bf16[1,4096,512]{1,2,0:T(8,128)(2,1)S(1)}, bf16[1,4096,512]{1,2,0:T(8,128)(2,1)}, u32[]{:S(2)}) copy-start(bf16[1,4096,512]{1,2,0:T(8,128)(2,1)} %copy.23) | copy-start | bytes 12582916
  371.5 146.7 %reduce-scatter.17.cloned.1.call-start = ((), (), s32[]{:S(2)}) async-start(), calls=%async_computation.9 | async-start | bytes 1531904 | tf_op jit(solution)/shard_map/reduce_scatter | solution.py:53
  388.9 200.9 %reduce-scatter.15.cloned.1.call-start = ((), (), s32[]{:S(2)}) async-start(), calls=%async_computation.8 | async-start | bytes 1531904 | tf_op jit(solution)/shard_map/reduce_scatter | solution.py:53
  406.6 254.9 %reduce-scatter.21.cloned.1.call-start = ((), (), s32[]{:S(2)}) async-start(), calls=%async_computation.17 | async-start | bytes 1531904
  427.2 347.5 %copy-start.5 = (bf16[2,88,512]{2,1,0:T(8,128)(2,1)S(1)}, bf16[2,88,512]{2,1,0:T(8,128)(2,1)}, u32[]{:S(2)}) copy-start(bf16[2,88,512]{2,1,0:T(8,128)(2,1)} %param.15) | copy-start | bytes 540676
  427.2 347.5 %copy-start.6 = (f32[2,88,512]{2,1,0:T(8,128)S(1)}, f32[2,88,512]{2,1,0:T(8,128)}, u32[]{:S(2)}) copy-start(f32[2,88,512]{2,1,0:T(8,128)} %param.21) | copy-start | bytes 1081348
  427.2 347.5 %copy-start.7 = (f32[2,88,512]{2,1,0:T(8,128)S(1)}, f32[2,88,512]{2,1,0:T(8,128)}, u32[]{:S(2)}) copy-start(f32[2,88,512]{2,1,0:T(8,128)} %param.18) | copy-start | bytes 1081348
  427.2 349.4 %copy-start.3 = (bf16[2,32,1408]{2,1,0:T(8,128)(2,1)S(1)}, bf16[2,32,1408]{2,1,0:T(8,128)(2,1)}, u32[]{:S(2)}) copy-start(bf16[2,32,1408]{2,1,0:T(8,128)(2,1)} %param.13) | copy-start | bytes 540676
  427.2 349.4 %copy-start.4 = (bf16[2,32,1408]{2,1,0:T(8,128)(2,1)S(1)}, bf16[2,32,1408]{2,1,0:T(8,128)(2,1)}, u32[]{:S(2)}) copy-start(bf16[2,32,1408]{2,1,0:T(8,128)(2,1)} %param.14) | copy-start | bytes 540676
  427.2 349.4 %copy-start.8 = (f32[2,32,1408]{2,1,0:T(8,128)S(1)}, f32[2,32,1408]{2,1,0:T(8,128)}, u32[]{:S(2)}) copy-start(f32[2,32,1408]{2,1,0:T(8,128)} %param.19) | copy-start | bytes 1081348
  427.2 349.4 %copy-start.9 = (f32[2,32,1408]{2,1,0:T(8,128)S(1)}, f32[2,32,1408]{2,1,0:T(8,128)}, u32[]{:S(2)}) copy-start(f32[2,32,1408]{2,1,0:T(8,128)} %param.16) | copy-start | bytes 1081348
  427.3 349.4 %copy-start.10 = (f32[2,32,1408]{2,1,0:T(8,128)S(1)}, f32[2,32,1408]{2,1,0:T(8,128)}, u32[]{:S(2)}) copy-start(f32[2,32,1408]{2,1,0:T(8,128)} %param.20) | copy-start | bytes 1081348
  427.3 349.4 %copy-start.11 = (f32[2,32,1408]{2,1,0:T(8,128)S(1)}, f32[2,32,1408]{2,1,0:T(8,128)}, u32[]{:S(2)}) copy-start(f32[2,32,1408]{2,1,0:T(8,128)} %param.17) | copy-start | bytes 1081348
  427.3 305.7 %reduce-scatter.19.cloned.1.call-start = ((), (), s32[]{:S(2)}) async-start(), calls=%async_computation.16 | async-start | bytes 1531904
  (5 other events, 33.8 us)
Sparse Core Ops, SparseCore 0:
  10.6 40.7 all-gather.12
  54.0 37.5 all-gather.14
  94.1 37.5 all-gather.16
  134.2 37.5 all-gather.20
  174.2 37.5 all-gather.22
  214.2 37.5 all-gather.18
  306.1 68.6 reduce-scatter.12
  377.8 68.6 reduce-scatter.10
  449.6 68.6 reduce-scatter.16
  521.2 68.5 reduce-scatter.14
  592.9 68.5 reduce-scatter.20
  664.4 68.5 reduce-scatter.18
where the time goes:
time: 796 us; the launch traced here: 786 us
  waiting for transfers between devices  437 us (55%)
  matrix products  259 us (33%)
  blocking collectives  38.7 us (5%)
  local copies, waits for them, and re-layouts  18.2 us (2%)
  between operations  17.3 us (2%)
  other arithmetic  15.2 us (2%)
    reduce_scatter x4, waiting for transfers between devices, step(): lax.psum_scatter(by_w[name], 'dp', scatter_dimension=0, tiled=True)  148 us
    all_gather x6, waiting for transfers between devices, fetched(): lax.all_gather(w[number], 'dp', axis=0, tiled=True)  146 us
    unnamed x14, waiting for transfers between devices  142 us
    dot_general x5, matrix products, layer(): gate = jnp.dot(a, w['w_gate'], preferred_element_type=jnp.float32)  103 us
    dot_general x5, matrix products, layer(): up = jnp.dot(a, w['w_up'], preferred_element_type=jnp.float32)  89.4 us
    dot_general x5, matrix products, matmul(): jnp.dot(a, w, preferred_element_type=jnp.float32).astype(jnp.bfloat16)  66.6 us
    psum x1, blocking collectives, step(): squares = lax.psum(sum((jnp.sum(g * g) for g in gradients)), 'dp')  38.7 us
  transfers between devices with their start and end apart: 12, of which 11 were waited for; matrix products, arithmetic and copies ran while one was open for 29% of the time, Pallas kernels for 0%

commit v1 on v0

v1 whole, which is shorter than its diff:
```python
import functools

import jax
import jax.numpy as jnp
from jax import lax
from jax.experimental import pallas as pl
from jax.experimental.pallas import tpu as pltpu
from jax.sharding import PartitionSpec as P

F32, BF = jnp.float32, jnp.bfloat16
MESH = pl.DeviceIdType.MESH
LANE = 128
TILE = 512
SIDE = 4
STEPS = "ABCD"


def dot(a, b, ca=1, cb=0):
    return lax.dot_general(a, b, (((ca,), (cb,)), ((), ())), preferred_element_type=F32)


def inverse_rms(wide):
    return lax.rsqrt(jnp.mean(wide * wide, -1, keepdims=True) + 1e-6)


def place():
    me = lax.axis_index("dp")
    return me // SIDE, lax.rem(me, SIDE)


def shifted(i, by):
    return lax.rem(i + by + SIDE, SIDE)


def along(order, by, second=False):
    x, y = place()
    if (order == "y") != second:
        return {"dp": x * SIDE + shifted(y, by)}
    return {"dp": shifted(x, by) * SIDE + y}


def ring_places(order):
    x, y = place()
    return (y, x) if order == "y" else (x, y)


def entry_barrier(peers):
    barrier = pltpu.get_barrier_semaphore()
    for peer in peers:
        pl.semaphore_signal(barrier, inc=1, device_id=peer, device_id_type=MESH)
    pl.semaphore_wait(barrier, len(peers))


def neighbours():
    return [along("y", 1), along("y", -1), along("x", 1), along("x", -1)]


class Gather:
    def __init__(self, buf, core, cut, rows, send, recv, base):
        self.buf, self.core, self.send, self.recv, self.base = buf, core, send, recv, base
        half = buf.shape[-1] // 2
        self.half, self.rows, self.r = half, rows, buf.shape[-2]
        self.columns = {"y": (0, cut), "x": (cut, half - cut)}

    def at(self, order, first, second, rows=slice(None)):
        off, width = self.columns[order]
        cols = pl.ds(pl.multiple_of(self.core * self.half + off, LANE), width)
        a, b = (second, first) if order == "y" else (first, second)
        return self.buf.at[a, b, rows, cols]

    def copies(self, step):
        out = []
        for which, order in enumerate("yx"):
            i1, i2 = ring_places(order)
            if step == "A":
                refs = [self.at(order, i1, i2)] * 2
            elif step == "B":
                refs = [
                    self.at(order, shifted(i1, -1), i2, pl.ds(0, self.rows)),
                    self.at(order, shifted(i1, 1), i2, pl.ds(self.rows, self.r - self.rows)),
                ]
            elif step == "C":
                refs = [self.at(order, slice(None), i2)] * 2
            else:
                refs = [
                    self.at(order, pl.ds(0, SIDE // 2), shifted(i2, -1)),
                    self.at(order, pl.ds(SIDE // 2, SIDE // 2), shifted(i2, 1)),
                ]
            for side, ref in enumerate(refs):
                number = self.base + STEPS.index(step) * 4 + which * 2 + side
                out.append(
                    pltpu.make_async_remote_copy(
                        src_ref=ref,
                        dst_ref=ref,
                        send_sem=self.send.at[number],
                        recv_sem=self.recv.at[number],
                        device_id=along(order, 1 - 2 * side, step in "CD"),
                        device_id_type=MESH,
                    )
                )
        return out

    def across(self, partner):
        ref = self.buf.at[:, :, :, pl.ds(pl.multiple_of(self.core * self.half, LANE), self.half)]
        number = self.base + 16
        return pltpu.make_async_remote_copy(
            src_ref=ref, dst_ref=ref, send_sem=self.send.at[number], recv_sem=self.recv.at[number], device_id=partner, device_id_type=MESH
        )

    def advance(self, step, partner):
        if step != "A":
            for copy in self.copies("ABCDE"["ABCDE".index(step) - 1]):
                copy.wait_recv()
        if step == "E":
            self.across(partner).start()
        else:
            for copy in self.copies(step):
                copy.start()

    def finish(self, partner):
        self.across(partner).wait_recv()

    def drain(self, partner):
        for step in STEPS:
            for copy in self.copies(step):
                copy.wait_send()
        self.across(partner).wait_send()


def forward_kernel(layers, wg_ref, wu_ref, wd_ref, x_ref, h_ref, *refs):
    (ogu, od), (gu, dd, wide_d, wd0, send, recv, out_sem) = (refs[:layers], refs[layers : 2 * layers]), refs[2 * layers :]
    step, steps = pl.program_id(0), pl.num_programs(0)
    ff = wg_ref.shape[2]
    rep = lax.axis_index("rep")
    core = lax.rem(rep, 2)
    partner = {"rep": rep + 1 - 2 * core}
    x, y = place()
    units = []
    for layer in range(layers):
        n = 2 * layer
        units.append(Gather(gu.at[layer], core, (gu.shape[-1] // 4 + LANE - 1) // LANE * LANE, 16, send, recv, 17 * n))
        units.append(Gather(dd.at[layer], core, dd.shape[-1] // 4, 48, send, recv, 17 * (n + 1)))
    first, rest = units[:2], units[2:]

    def outs(layer):
        return [
            pltpu.make_async_copy(gu.at[layer], ogu[layer], out_sem.at[2 * layer]),
            pltpu.make_async_copy(dd.at[layer], od[layer], out_sem.at[2 * layer + 1]),
        ]

    @pl.when(step == 0)
    def _():
        for layer in range(layers):
            for k in range(0, ff, LANE):
                gu[layer, x, y, :, 2 * k : 2 * k + LANE] = wg_ref[layer, :, k : k + LANE]
                gu[layer, x, y, :, 2 * k + LANE : 2 * k + 2 * LANE] = wu_ref[layer, :, k : k + LANE]
            dd[layer, x, y] = wd_ref[layer]
        entry_barrier(neighbours() + [partner])
        for letter in "ABCDE":
            for unit in first:
                unit.advance(letter, partner)
        for unit in rest:
            unit.advance("A", partner)
        for unit in first:
            unit.finish(partner)
        for copy in outs(0):
            copy.start()
        r = dd.shape[3]
        for d in range(SIDE * SIDE):
            wide_d[r * d : r * (d + 1)] = dd[0, d // SIDE, d % SIDE].astype(F32)
        wd0[...] = wide_d[...].astype(BF)

    for when, letter in ((1, "B"), (2, "C"), (4, "D"), (6, "E")):

        @pl.when(step == when)
        def _():
            for unit in rest:
                unit.advance(letter, partner)

    h = x_ref[...]
    wide = h.astype(F32)
    a = (wide * inverse_rms(wide)).astype(BF)
    total = jnp.zeros(h.shape, F32)
    w = gu.at[0]
    for j in range(0, ff, 2 * LANE):
        c = min(2 * LANE, ff - j)
        both = dot(a, w[:, :, :, 2 * j : 2 * (j + c)].reshape(h.shape[1], 2 * c))
        products = []
        for k in range(0, c, LANE):
            g, u = both[:, 2 * k : 2 * k + LANE], both[:, 2 * k + LANE : 2 * k + 2 * LANE]
            products.append((g * jax.nn.sigmoid(g) * u).astype(BF))
        total += dot(jnp.concatenate(products, 1), wd0[j : j + c, :])
    h_ref[...] = h + total.astype(BF)

    @pl.when(step == steps - 1)
    def _():
        for unit in rest:
            unit.finish(partner)
        for layer in range(1, layers):
            for copy in outs(layer):
                copy.start()
        for unit in units:
            unit.drain(partner)
        for layer in range(layers):
            for copy in outs(layer):
                copy.wait()


def forward(x, wg, wu, wd):
    tokens, d = x.shape
    layers, rows, ff = wg.shape
    rows_d = wd.shape[1]
    whole = lambda a: pl.BlockSpec(a.shape, lambda i: (0,) * a.ndim)
    h, *full = pl.pallas_call(
        functools.partial(forward_kernel, layers),
        grid=(tokens // TILE,),
        in_specs=[whole(wg), whole(wu), whole(wd), pl.BlockSpec((TILE, d), lambda i: (i, 0))],
        out_specs=[pl.BlockSpec((TILE, d), lambda i: (i, 0))] + [pl.BlockSpec(memory_space=pl.ANY)] * (2 * layers),
        out_shape=[jax.ShapeDtypeStruct((tokens, d), BF)]
        + [jax.ShapeDtypeStruct((SIDE, SIDE, rows, 2 * ff), BF)] * layers
        + [jax.ShapeDtypeStruct((SIDE, SIDE, rows_d, d), BF)] * layers,
        scratch_shapes=[
            pltpu.VMEM((layers, SIDE, SIDE, rows, 2 * ff), BF),
            pltpu.VMEM((layers, SIDE, SIDE, rows_d, d), BF),
            pltpu.VMEM((ff, d), F32),
            pltpu.VMEM((ff, d), BF),
            pltpu.SemaphoreType.DMA((2 * layers * 17,)),
            pltpu.SemaphoreType.DMA((2 * layers * 17,)),
            pltpu.SemaphoreType.DMA((2 * layers,)),
        ],
        compiler_params=pltpu.CompilerParams(collective_id=1, has_side_effects=True, vmem_limit_bytes=60 * 2**20),
    )(wg, wu, wd, x)
    return h, [one.reshape(d, 2 * ff) for one in full[:layers]], [one.reshape(ff, d) for one in full[layers:]]


def layer_kernel(through, h_ref, dy_ref, wgu_ref, wd_ref, *refs):
    if through:
        dh_ref, *refs = refs
    dwgu_ref, dwd_ref, accgu, accd, dgu, prod = refs
    step, steps = pl.program_id(0), pl.num_programs(0)
    ff = wd_ref.shape[0]

    @pl.when(step == 0)
    def _():
        accgu[...] = jnp.zeros_like(accgu)
        accd[...] = jnp.zeros_like(accd)

    wide = h_ref[...].astype(F32)
    scale = inverse_rms(wide)
    a = (wide * scale).astype(BF)
    dy = dy_ref[...]
    for j in range(0, ff, 2 * LANE):
        c = min(2 * LANE, ff - j)
        both = dot(a, wgu_ref[:, 2 * j : 2 * (j + c)])
        by = dot(dy, wd_ref[j : j + c, :], 1, 1).astype(BF).astype(F32)
        for k in range(0, c, LANE):
            g, u, b = both[:, 2 * k : 2 * k + LANE], both[:, 2 * k + LANE : 2 * k + 2 * LANE], by[:, k : k + LANE]
            s = jax.nn.sigmoid(g)
            silu = g * s
            at = j + k
            prod[:, at : at + LANE] = (silu * u).astype(BF)
            dgu[:, 2 * at : 2 * at + LANE] = (b * u * (s + silu * (1 - s))).astype(BF)
            dgu[:, 2 * at + LANE : 2 * at + 2 * LANE] = (b * silu).astype(BF)
    if through:
        da = dot(dgu[...], wgu_ref[...], 1, 1)
        back = scale * (da - wide * (scale * scale * jnp.mean(da * wide, -1, keepdims=True)))
        dh_ref[...] = dy + back.astype(BF)
    accgu[...] += dot(a, dgu[...], 0, 0)
    accd[...] += dot(prod[...], dy, 0, 0)

    @pl.when(step == steps - 1)
    def _():
        r, q = dwgu_ref.shape[2], dwd_ref.shape[2]
        for d in range(SIDE * SIDE):
            dwgu_ref[d // SIDE, d % SIDE] = accgu[r * d : r * (d + 1)].astype(BF)
            dwd_ref[d // SIDE, d % SIDE] = accd[q * d : q * (d + 1)].astype(BF)


def layer_back(through, h, dy, wgu, wd):
    tokens, d = h.shape
    ff = wd.shape[0]
    n = SIDE * SIDE
    tile = pl.BlockSpec((TILE, d), lambda i: (i, 0))
    whole = lambda shape: pl.BlockSpec(shape, lambda i: (0,) * len(shape))
    gu, dd = (SIDE, SIDE, d // n, 2 * ff), (SIDE, SIDE, ff // n, d)
    out_specs, out_shape = [whole(gu), whole(dd)], [jax.ShapeDtypeStruct(gu, BF), jax.ShapeDtypeStruct(dd, BF)]
    if through:
        out_specs, out_shape = [tile] + out_specs, [jax.ShapeDtypeStruct((tokens, d), BF)] + out_shape
    return pl.pallas_call(
        functools.partial(layer_kernel, through),
        grid=(tokens // TILE,),
        in_specs=[tile, tile, whole(wgu.shape), whole(wd.shape)],
        out_specs=out_specs,
        out_shape=out_shape,
        scratch_shapes=[
            pltpu.VMEM((d, 2 * ff), F32),
            pltpu.VMEM((ff, d), F32),
            pltpu.VMEM((TILE, 2 * ff), BF),
            pltpu.VMEM((TILE, ff), BF),
        ],
        compiler_params=pltpu.CompilerParams(vmem_limit_bytes=60 * 2**20),
    )(h, dy, wgu, wd)


class Scatter:
    def __init__(self, terms, bufs, send, recv, base):
        self.terms, self.send, self.recv, self.base = terms, send, recv, base
        self.a, self.b, self.sums, self.out, self.c, self.d = bufs
        self.half = terms.shape[-1] // 2
        r = terms.shape[2]
        if r % 32 == 0:
            self.parts = [(pl.ds(0, r // 2), slice(None)), (pl.ds(r // 2, r // 2), slice(None))]
        else:
            q = self.half // 2
            self.parts = [(slice(None), pl.ds(0, q)), (slice(None), pl.ds(q, q))]

    @staticmethod
    def scratch(rows, columns):
        half = columns // 2
        return [
            pltpu.VMEM((2, 2, SIDE // 2, rows, half), BF),
            pltpu.VMEM((2, 2, SIDE, rows, half), BF),
            pltpu.VMEM((2, SIDE, rows, half), F32),
            pltpu.VMEM((2, SIDE, rows, half), BF),
            pltpu.VMEM((2, rows, half), BF),
            pltpu.VMEM((2, 2, rows, half), BF),
        ]

    def index(self, which, first, second):
        cols = pl.ds(which * self.half, self.half)
        return (second, first, slice(None), cols) if which == 0 else (first, second, slice(None), cols)

    def copies(self, step):
        out = []
        for which, order in enumerate("yx"):
            i1, i2 = ring_places(order)
            for side in range(2):
                by = 1 - 2 * side
                if step == "A":
                    src = self.terms.at[self.index(which, shifted(i1, 2), pl.ds(side * (SIDE // 2), SIDE // 2))]
                    dst = self.a.at[which, side]
                elif step == "B":
                    src = self.terms.at[self.index(which, shifted(i1, by), slice(None))]
                    dst = self.b.at[which, side]
                elif step == "C":
                    rows, cols = self.parts[side]
                    src = self.out.at[which, shifted(i2, 2), rows, cols]
                    dst = self.c.at[which, rows, cols]
                else:
                    src = self.out.at[which, shifted(i2, by)]
                    dst = self.d.at[which, side]
                number = self.base + STEPS.index(step) * 4 + which * 2 + side
                out.append(
                    pltpu.make_async_remote_copy(
                        src_ref=src,
                        dst_ref=dst,
                        send_sem=self.send.at[number],
                        recv_sem=self.recv.at[number],
                        device_id=along(order, by, step in "CD"),
                        device_id_type=MESH,
                    )
                )
        return out

    def advance(self, step):
        if step != "A":
            for copy in self.copies("ABCD"["ABCDE".index(step) - 1]):
                copy.wait_recv()
        for which, order in enumerate("yx"):
            i1, i2 = ring_places(order)
            if step == "B":
                for side in range(2):
                    for k in range(SIDE // 2):
                        at = self.index(which, shifted(i1, 1 - 2 * side), side * (SIDE // 2) + k)
                        self.terms[at] = (self.terms[at].astype(F32) + self.a[which, side, k].astype(F32)).astype(BF)
            elif step == "C":

                def own(k, _):
                    mine = self.terms[self.index(which, i1, k)].astype(F32)
                    self.sums[which, k] = mine + self.b[which, 0, k].astype(F32) + self.b[which, 1, k].astype(F32)
                    return 0

                lax.fori_loop(0, SIDE, own, 0)
                far = shifted(i2, 2)
                self.out[which, far] = self.sums[which, far].astype(BF)
            elif step == "D":
                for side in range(2):
                    near = shifted(i2, 1 - 2 * side)
                    for part in range(2):
                        at = self.parts[part]
                        value = self.sums[(which, near) + at]
                        if part == side:
                            value = value + self.c[(which,) + at].astype(F32)
                        self.out[(which, near) + at] = value.astype(BF)
        if step != "E":
            for copy in self.copies(step):
                copy.start()

    def result(self):
        halves = []
        for which, order in enumerate("yx"):
            _, i2 = ring_places(order)
            total = self.sums[which, i2] + self.d[which, 0].astype(F32) + self.d[which, 1].astype(F32)
            halves.append(total.astype(BF))
        return halves

    def drain(self):
        for step in STEPS:
            for copy in self.copies(step):
                copy.wait_send()


def sum_everywhere(value, mine, theirs, send, recv, base):
    for which, order in enumerate("yx"):
        mine[which] = jnp.broadcast_to(value, mine.shape[1:])
        copies = [
            pltpu.make_async_remote_copy(
                src_ref=mine.at[which],
                dst_ref=theirs.at[which, by - 1],
                send_sem=send.at[base + which * 3 + by - 1],
                recv_sem=recv.at[base + which * 3 + by - 1],
                device_id=along(order, by),
                device_id_type=MESH,
            )
            for by in range(1, SIDE)
        ]
        for copy in copies:
            copy.start()
        for copy in copies:
            copy.wait()
        value = value + theirs[which, 0][:1, :1] + theirs[which, 1][:1, :1] + theirs[which, 2][:1, :1]
    return value


def reduce_kernel(layers, *refs):
    gus, dds, (rg, ru, rd, total), refs = refs[:layers], refs[layers : 2 * layers], refs[2 * layers : 2 * layers + 4], refs[2 * layers + 4 :]
    terms, refs = refs[: 2 * layers], refs[2 * layers :]
    bufs, (mine, theirs, send, recv, load) = refs[: 12 * layers], refs[12 * layers :]
    units = [Scatter(terms[n], bufs[6 * n : 6 * n + 6], send, recv, 16 * n) for n in range(2 * layers)]
    sources = [one for layer in reversed(range(layers)) for one in (gus[layer], dds[layer])]
    loads = [pltpu.make_async_copy(source, term, load.at[n]) for n, (source, term) in enumerate(zip(sources, terms, strict=True))]
    for copy in loads:
        copy.start()
    entry_barrier(neighbours() + [along("y", 2), along("x", 2)])
    for copy, unit in zip(loads, units, strict=True):
        copy.wait()
        unit.advance("A")
    for letter in "BCDE":
        for unit in units:
            unit.advance(letter)
    squares = jnp.zeros((1, 1), F32)
    for n, unit in enumerate(units):
        layer = layers - 1 - n // 2
        for which, half in enumerate(unit.result()):
            wide = half.astype(F32)
            squares += jnp.sum(wide * wide, keepdims=True)
            width = half.shape[1]
            if n % 2:
                rd[layer, :, which * width : (which + 1) * width] = half
            else:
                for k in range(0, width, LANE):
                    block = (which * width + k) // LANE
                    out = (rg, ru)[block % 2]
                    out[layer, :, block // 2 * LANE : (block // 2 + 1) * LANE] = half[:, k : k + LANE]
    total[...] = jnp.broadcast_to(sum_everywhere(squares, mine, theirs, send, recv, 16 * len(units)), total.shape)
    for unit in units:
        unit.drain()


def reduced(gus, dds):
    layers = len(gus)
    rows, ff = gus[0].shape[2], gus[0].shape[3] // 2
    rows_d, d = dds[0].shape[2:]
    shapes = [one.shape for _ in range(layers) for one in (gus[0], dds[0])]
    scratch = [pltpu.VMEM(shape, BF) for shape in shapes]
    for shape in shapes:
        scratch += Scatter.scratch(shape[2], shape[3])
    n = 16 * len(shapes) + 6
    return pl.pallas_call(
        functools.partial(reduce_kernel, layers),
        in_specs=[pl.BlockSpec(memory_space=pl.ANY)] * (2 * layers),
        out_specs=[pl.BlockSpec(memory_space=pltpu.VMEM)] * 4,
        out_shape=[
            jax.ShapeDtypeStruct((layers, rows, ff), BF),
            jax.ShapeDtypeStruct((layers, rows, ff), BF),
            jax.ShapeDtypeStruct((layers, rows_d, d), BF),
            jax.ShapeDtypeStruct((8, LANE), F32),
        ],
        scratch_shapes=scratch
        + [
            pltpu.VMEM((2, 8, LANE), F32),
            pltpu.VMEM((2, SIDE - 1, 8, LANE), F32),
            pltpu.SemaphoreType.DMA((n,)),
            pltpu.SemaphoreType.DMA((n,)),
            pltpu.SemaphoreType.DMA((len(shapes),)),
        ],
        compiler_params=pltpu.CompilerParams(collective_id=2, has_side_effects=True, vmem_limit_bytes=60 * 2**20),
    )(*gus, *dds)


def adamw(w, m, v, g):
    m = 0.9 * m + 0.1 * g
    v = 0.95 * v + 0.05 * g * g
    step = m * lax.rsqrt(v + 1e-8) + 0.1 * w
    return (w - 0.02 * step).astype(jnp.bfloat16), m, v


def solution(mesh):
    group = mesh.shape["dp"]

    def step(x, dy, *arrays):
        weights, m, v = (arrays[i : i + 3] for i in (0, 3, 6))
        h0, by1 = x[0], dy[0]
        h1, wgu, wd = forward(h0, *weights)
        by0, gu1, dd1 = layer_back(True, h1, by1, wgu[1], wd[1])
        gu0, dd0 = layer_back(False, h0, by0, wgu[0], wd[0])
        *gradients, total = reduced([gu0, gu1], [dd0, dd1])
        count = group * sum(g.size for g in gradients)
        factor = jnp.minimum(1.0, 0.5 * lax.rsqrt(total[0, 0] / count + 1e-30))
        new = [adamw(w.astype(F32), m, v, g.astype(F32) * factor) for w, m, v, g in zip(weights, m, v, gradients, strict=True)]
        return tuple(one[which] for which in range(3) for one in new)

    states, cut = P(("rep", "dp"), None, None), P(None, "dp", None)
    return jax.shard_map(
        step,
        mesh=mesh,
        in_specs=(states, states) + (cut,) * 9,
        out_specs=(P("rep", "dp", None),) * 9,
        check_vma=False,
    )
```

time: 796 us -> 230 us (0.29); the launches traced: 786 us -> 229 us
  waiting for transfers between devices: 437 us -> 0 us
  matrix products: 259 us -> 0 us
  Pallas kernels: 0 us -> 222 us
  blocking collectives: 38.7 us -> 0 us
  local copies, waits for them, and re-layouts: 18.2 us -> 1.24 us
  between operations: 17.3 us -> 1.46 us
  other arithmetic: 15.2 us -> 4.34 us
    dot_general x15 -> x0, matrix products: 259 us -> none  [the longest x5 103 us: layer(): gate = jnp.dot(a, w['w_gate'], preferred_element_type=jnp.float32)]
    pallas_call x0 -> x4, Pallas kernels: none -> 222 us  [the longest x2 108 us: layer_back(): pl.pallas_call(functools.partial(layer_kernel, through), grid=(tokens //...]
    reduce_scatter x4 -> x0, waiting for transfers between devices: 148 us -> none  [step(): lax.psum_scatter(by_w[name], 'dp', scatter_dimension=0, tiled=True)]
    all_gather x6 -> x0, waiting for transfers between devices: 146 us -> none  [fetched(): lax.all_gather(w[number], 'dp', axis=0, tiled=True)]
    unnamed x14 -> x0, waiting for transfers between devices: 142 us -> none
    psum x1 -> x0, blocking collectives: 38.7 us -> none  [step(): squares = lax.psum(sum((jnp.sum(g * g) for g in gradients)), 'dp')]
    unnamed x36 -> x18, local copies, waits for them, and re-layouts: 13.4 us -> 0.05 us
    reduce_sum x4 -> x0, other arithmetic: 7.96 us -> none  [the longest x3 4.89 us: step(): squares = lax.psum(sum((jnp.sum(g * g) for g in gradients)), 'dp')]
  transfers between devices with their start and end apart: 12 -> 0, of which waited for: 11 -> 0; matrix products, arithmetic and copies ran while one was open for 29% -> 0% of each run, Pallas kernels for 0% -> 0%
where the time goes in v1:
time: 230 us; the launch traced here: 229 us
  Pallas kernels  222 us (97%)
  other arithmetic  4.34 us (2%)
    pallas_call x2, Pallas kernels, layer_back(): pl.pallas_call(functools.partial(layer_kernel, through), grid=(tokens //...  108 us
    pallas_call x1, Pallas kernels, reduced(): pl.pallas_call(functools.partial(reduce_kernel, layers), in_specs=[pl.Blo...  58.3 us
    pallas_call x1, Pallas kernels, forward(): pl.pallas_call(functools.partial(forward_kernel, layers), grid=(tokens //...  56.3 us

profile of v1, /device:TPU:96, one launch (start us, length us, event | category | flops | bytes accessed | tf_op | source)
XLA Modules:
  0.0 229.3 jit_solution(15564467663769208454)
XLA Ops:
  0.6 56.3 %shard_map.178 = (bf16[4096,512]{1,0:T(8,128)(2,1)}, bf16[4,4,32,2816]{3,2,1,0:T(8,128)(2,1)}, bf16[4,4,32,2816]{3,2,1,0:T(8,128)(2,1)}, bf16[4,4,88,512]{3,2,1,0:T(8,128)(2,1)}, bf16[4,4,88,512]{3,2,1,0:T(8,128)(2,1)}) custom-call(bf16[2,32,1408]{2,1,0:T(8,128)(2,1)} %wg_ref.1, bf16[2,32,1408]{2,1,0:T(8,128)(2,1)} %wu_ref.1, bf16[2,88,512]{2,1,0:T(8,128)(2,1)} %wd_ref.1, ...), custom_call_target="tpu_custom_call" | custom-call | tf_op jit(solution)/shard_map/pallas_call | solution.py:214
  57.0 59.9 %shard_map.179 = (bf16[4096,512]{1,0:T(8,128)(2,1)}, bf16[4,4,32,2816]{3,2,1,0:T(8,128)(2,1)}, bf16[4,4,88,512]{3,2,1,0:T(8,128)(2,1)}) custom-call(bf16[4096,512]{1,0:T(8,128)(2,1)} %get-tuple-element.23.h_ref, bf16[4096,512]{1,0:T(8,128)(2,1)} %bitcast.9, bf16[512,2816]{1,0:T(8,128)(2,1)} %bitcast.11, bf16[1408,512]{1,0:T(8,128)(2,1)} %bitcast.13), custom_call_target="tpu_custom_call" | custom-call | tf_op jit(solution)/shard_map/pallas_call | solution.py:289
  116.9 47.7 %shard_map.180 = (bf16[4,4,32,2816]{3,2,1,0:T(8,128)(2,1)}, bf16[4,4,88,512]{3,2,1,0:T(8,128)(2,1)}) custom-call(bf16[4096,512]{1,0:T(8,128)(2,1)} %bitcast.8, bf16[4096,512]{1,0:T(8,128)(2,1)} %get-tuple-element.26.dy_ref, bf16[512,2816]{1,0:T(8,128)(2,1)} %bitcast.10, bf16[1408,512]{1,0:T(8,128)(2,1)} %bitcast.12), custom_call_target="tpu_custom_call" | custom-call | tf_op jit(solution)/shard_map/pallas_call | solution.py:289
  164.6 0.0 copy-start.2
  164.6 0.0 copy-start.3
  164.6 0.0 copy-start
  164.6 0.0 copy-start.1
  164.6 0.0 copy-start.5
  164.6 0.0 copy-start.6
  164.6 0.0 copy-start.7
  164.7 0.0 copy-start.8
  164.7 58.3 %shard_map.181 = (bf16[2,32,1408]{2,1,0:T(8,128)(2,1)}, bf16[2,32,1408]{2,1,0:T(8,128)(2,1)}, bf16[2,88,512]{2,1,0:T(8,128)(2,1)}, f32[8,128]{1,0:T(8,128)}) custom-call(bf16[4,4,32,2816]{3,2,1,0:T(8,128)(2,1)} %get-tuple-element.29.refs_0_, bf16[4,4,32,2816]{3,2,1,0:T(8,128)(2,1)} %get-tuple-element.30.refs_1_, ...), custom_call_target="tpu_custom_call" | custom-call | tf_op jit(solution)/shard_map/pallas_call | solution.py:479
  223.0 1.2 slice.3
  224.8 0.0 copy-done.2
  224.9 0.0 copy-done.3
  224.9 0.0 copy-done.4
  224.9 1.9 fusion.8
  226.8 0.0 copy-done
  226.8 0.0 copy-done.1
  226.8 0.0 copy-done.5
  226.8 0.0 copy-done.6
  226.8 0.0 copy-done.7
  226.8 0.0 copy-done.8
  226.8 2.4 %fusion.2 = (bf16[2,32,1408]{2,1,0:T(8,128)(2,1)}, f32[2,32,1408]{2,1,0:T(8,128)}, f32[2,32,1408]{2,1,0:T(8,128)}, bf16[2,32,1408]{2,1,0:T(8,128)(2,1)}, f32[2,32,1408]{2,1,0:T(8,128)}, /*index=5*/f32[2,32,1408]{2,1,0:T(8,128)}) fusion(bf16[2,32,1408]{2,1,0:T(8,128)(2,1)S(1)} %copy-done, f32[]{:T(128)} %bitcast.6, ...), kind=kLoop, calls=%fused_computation.11 | loop fusion | flops 3063808 | bytes 3964932 | tf_op jit(solution)/shard_map/convert_element_type | solution.py:505
  (1 shorter events, 0.0 us)
Async XLA Ops:
  164.6 60.3 %copy-start.2 = (bf16[2,88,512]{2,1,0:T(8,128)(2,1)S(1)}, bf16[2,88,512]{2,1,0:T(8,128)(2,1)}, u32[]{:S(2)}) copy-start(bf16[2,88,512]{2,1,0:T(8,128)(2,1)} %wd_ref.1) | copy-start | bytes 540676
  164.6 60.3 %copy-start.3 = (f32[2,88,512]{2,1,0:T(8,128)S(1)}, f32[2,88,512]{2,1,0:T(8,128)}, u32[]{:S(2)}) copy-start(f32[2,88,512]{2,1,0:T(8,128)} %param.21) | copy-start | bytes 1081348
  164.6 60.3 %copy-start.4 = (f32[2,88,512]{2,1,0:T(8,128)S(1)}, f32[2,88,512]{2,1,0:T(8,128)}, u32[]{:S(2)}) copy-start(f32[2,88,512]{2,1,0:T(8,128)} %param.18) | copy-start | bytes 1081348
  164.6 62.2 %copy-start = (bf16[2,32,1408]{2,1,0:T(8,128)(2,1)S(1)}, bf16[2,32,1408]{2,1,0:T(8,128)(2,1)}, u32[]{:S(2)}) copy-start(bf16[2,32,1408]{2,1,0:T(8,128)(2,1)} %wg_ref.1) | copy-start | bytes 540676
  164.6 62.2 %copy-start.1 = (bf16[2,32,1408]{2,1,0:T(8,128)(2,1)S(1)}, bf16[2,32,1408]{2,1,0:T(8,128)(2,1)}, u32[]{:S(2)}) copy-start(bf16[2,32,1408]{2,1,0:T(8,128)(2,1)} %wu_ref.1) | copy-start | bytes 540676
  164.6 62.2 %copy-start.5 = (f32[2,32,1408]{2,1,0:T(8,128)S(1)}, f32[2,32,1408]{2,1,0:T(8,128)}, u32[]{:S(2)}) copy-start(f32[2,32,1408]{2,1,0:T(8,128)} %param.19) | copy-start | bytes 1081348
  164.6 62.2 %copy-start.6 = (f32[2,32,1408]{2,1,0:T(8,128)S(1)}, f32[2,32,1408]{2,1,0:T(8,128)}, u32[]{:S(2)}) copy-start(f32[2,32,1408]{2,1,0:T(8,128)} %param.16) | copy-start | bytes 1081348
  164.6 62.2 %copy-start.7 = (f32[2,32,1408]{2,1,0:T(8,128)S(1)}, f32[2,32,1408]{2,1,0:T(8,128)}, u32[]{:S(2)}) copy-start(f32[2,32,1408]{2,1,0:T(8,128)} %param.20) | copy-start | bytes 1081348
  164.7 62.2 %copy-start.8 = (f32[2,32,1408]{2,1,0:T(8,128)S(1)}, f32[2,32,1408]{2,1,0:T(8,128)}, u32[]{:S(2)}) copy-start(f32[2,32,1408]{2,1,0:T(8,128)} %param.17) | copy-start | bytes 1081348

commit v2 on v1

v2 whole, which is shorter than its diff:
```python
import functools

import jax
import jax.numpy as jnp
from jax import lax
from jax.experimental import pallas as pl
from jax.experimental.pallas import tpu as pltpu
from jax.sharding import PartitionSpec as P

F32, BF = jnp.float32, jnp.bfloat16
MESH = pl.DeviceIdType.MESH
LANE = 128
TILE = 512
FORWARD_TILE = 1024
BACK_TILE = 1024
SIDE = 4
HOPS = (1, -1, 2)


def dot(a, b, ca=1, cb=0):
    return lax.dot_general(a, b, (((ca,), (cb,)), ((), ())), preferred_element_type=F32)


def inverse_rms(wide):
    return lax.rsqrt(jnp.mean(wide * wide, -1, keepdims=True) + 1e-6)


def place():
    me = lax.axis_index("dp")
    return me // SIDE, lax.rem(me, SIDE)


def others():
    return [along(order, by) for order in "yx" for by in HOPS]


def shifted(i, by):
    return lax.rem(i + by + SIDE, SIDE)


def along(order, by, second=False):
    x, y = place()
    if (order == "y") != second:
        return {"dp": x * SIDE + shifted(y, by)}
    return {"dp": shifted(x, by) * SIDE + y}


def ring_places(order):
    x, y = place()
    return (y, x) if order == "y" else (x, y)


def entry_barrier(peers):
    with jax.named_scope("entry"):
        barrier = pltpu.get_barrier_semaphore()
        for peer in peers:
            pl.semaphore_signal(barrier, inc=1, device_id=peer, device_id_type=MESH)
        pl.semaphore_wait(barrier, len(peers))


class Gather:
    def __init__(self, buf, core, cut, rows, send, recv, base, direct=False):
        self.steps = "ACE" if direct else "ABCDE"
        self.buf, self.core, self.send, self.recv, self.base = buf, core, send, recv, base
        half = buf.shape[-1] // 2
        self.half, self.rows, self.r = half, rows, buf.shape[-2]
        self.columns = {"y": (0, cut), "x": (cut, half - cut)}

    def at(self, order, first, second, rows=slice(None)):
        off, width = self.columns[order]
        cols = pl.ds(pl.multiple_of(self.core * self.half + off, LANE), width)
        a, b = (second, first) if order == "y" else (first, second)
        return self.buf.at[a, b, rows, cols]

    def copies(self, step):
        out = []
        for which, order in enumerate("yx"):
            i1, i2 = ring_places(order)
            hops = HOPS if self.steps == "ACE" else HOPS[:2]
            if step == "A":
                refs = [self.at(order, i1, i2)] * len(hops)
            elif step == "B":
                refs = [
                    self.at(order, shifted(i1, -1), i2, pl.ds(0, self.rows)),
                    self.at(order, shifted(i1, 1), i2, pl.ds(self.rows, self.r - self.rows)),
                ]
            elif step == "C":
                refs = [self.at(order, slice(None), i2)] * len(hops)
            else:
                refs = [
                    self.at(order, pl.ds(0, SIDE // 2), shifted(i2, -1)),
                    self.at(order, pl.ds(SIDE // 2, SIDE // 2), shifted(i2, 1)),
                ]
            for side, ref in enumerate(refs):
                number = self.base + self.steps.index(step) * 2 * len(hops) + which * len(hops) + side
                out.append(
                    pltpu.make_async_remote_copy(
                        src_ref=ref,
                        dst_ref=ref,
                        send_sem=self.send.at[number],
                        recv_sem=self.recv.at[number],
                        device_id=along(order, hops[side], step in "CD"),
                        device_id_type=MESH,
                    )
                )
        return out

    def across(self, partner):
        ref = self.buf.at[:, :, :, pl.ds(pl.multiple_of(self.core * self.half, LANE), self.half)]
        number = self.base + 16
        return pltpu.make_async_remote_copy(
            src_ref=ref, dst_ref=ref, send_sem=self.send.at[number], recv_sem=self.recv.at[number], device_id=partner, device_id_type=MESH
        )

    def advance(self, step, partner):
        if step != "A":
            with jax.named_scope(f"wait_{step}{self.base // 17}"):
                for copy in self.copies(self.steps[self.steps.index(step) - 1]):
                    copy.wait_recv()
        if step == "E":
            self.across(partner).start()
        else:
            for copy in self.copies(step):
                copy.start()

    def finish(self, partner):
        with jax.named_scope(f"wait_F{self.base // 17}"):
            self.across(partner).wait_recv()

    def drain(self, partner):
        for step in self.steps[:-1]:
            for copy in self.copies(step):
                copy.wait_send()
        self.across(partner).wait_send()


def pieces_of(ff):
    cuts = [0, 3 * LANE, 7 * LANE, ff]
    return list(zip(cuts[:-1], cuts[1:]))


def forward_kernel(layers, wg_ref, wu_ref, wd_ref, x_hbm, h_hbm, a_hbm, prod_hbm, *refs):
    (ogu, od), refs = (refs[:layers], refs[layers : 2 * layers]), refs[2 * layers :]
    ff = wg_ref.shape[2]
    pieces = pieces_of(ff)
    first, (later, dd, xv, a, prod, wide_d, wd0, send, recv, out_sem, h_sem, p_sem) = refs[: len(pieces)], refs[len(pieces) :]
    tokens, d = xv.shape
    tiles = tokens // FORWARD_TILE
    rep = lax.axis_index("rep")
    core = lax.rem(rep, 2)
    partner = {"rep": rep + 1 - 2 * core}
    x, y = place()
    x_load = pltpu.make_async_copy(x_hbm, xv, out_sem.at[0])
    x_load.start()

    def placed(buf, layer, start, stop):
        for k in range(start, stop, LANE):
            at = 2 * (k - start)
            buf[x, y, :, at : at + LANE] = wg_ref[layer, :, k : k + LANE]
            buf[x, y, :, at + LANE : at + 2 * LANE] = wu_ref[layer, :, k : k + LANE]

    bufs = list(first) + [dd.at[0]]
    for buf, (start, stop) in zip(first, pieces, strict=True):
        placed(buf, 0, start, stop)
    for layer in range(1, layers):
        placed(later.at[layer - 1], layer, 0, ff)
        bufs += [later.at[layer - 1], dd.at[layer]]
    for layer in range(layers):
        dd[layer, x, y] = wd_ref[layer]
    entry_barrier(others() + [partner])

    def unit_of(n, buf):
        quarter = (buf.shape[-1] // 4 + LANE - 1) // LANE * LANE
        return Gather(buf, core, quarter, 16 if buf.shape[2] % 32 == 0 else 48, send, recv, 17 * n, n == 0)

    units = [unit_of(n, buf) for n, buf in enumerate(bufs)]
    gus, down, rest = units[: len(pieces)], units[len(pieces)], units[len(pieces) + 1 :]
    one, two, three = gus

    def go(step, *those):
        for unit in those:
            unit.advance(step, partner)

    go("A", *gus, down)
    x_load.wait()

    def norm(t, _):
        rows = pl.ds(pl.multiple_of(t * FORWARD_TILE, FORWARD_TILE), FORWARD_TILE)
        wide = xv[rows].astype(F32)
        a[rows] = (wide * inverse_rms(wide)).astype(BF)
        return 0

    with jax.named_scope("norm"):
        lax.fori_loop(0, tiles, norm, 0)
    go("C", one)
    go("B", two, three, down)
    go("C", two)
    go("E", one)
    slots = [
        {2: [("D", [two]), ("C", [three])], 4: [("C", [down])], 6: [("E", [two]), ("D", [three]), ("A", rest)]},
        {0: [("D", [down])], 2: [("E", [three]), ("B", rest)], 4: [("E", [down]), ("C", rest)]},
        {},
    ]
    for unit, buf, (start, stop), slot in zip(gus, first, pieces, slots, strict=True):
        unit.finish(partner)

        def products(t, _):
            for when, actions in slot.items():

                @pl.when(t == when * tiles // 8)
                def _():
                    for step, those in actions:
                        go(step, *those)

            rows = pl.ds(pl.multiple_of(t * FORWARD_TILE, FORWARD_TILE), FORWARD_TILE)
            at = a[rows]
            for j in range(start, stop, 2 * LANE):
                c = min(2 * LANE, stop - j)
                w = buf[:, :, :, 2 * (j - start) : 2 * (j - start + c)].reshape(d, 2 * c)
                both = dot(at, w)
                for k in range(0, c, LANE):
                    g, u = both[:, 2 * k : 2 * k + LANE], both[:, 2 * k + LANE : 2 * k + 2 * LANE]
                    prod[rows, j + k : j + k + LANE] = (g * jax.nn.sigmoid(g) * u).astype(BF)
            return 0

        with jax.named_scope(f"products_{start}"):
            lax.fori_loop(0, tiles, products, 0)

    def gu_out(n):
        start, stop = pieces[n]
        return pltpu.make_async_copy(first[n], ogu[0].at[:, :, :, 2 * start : 2 * stop], out_sem.at[n])

    a_out = pltpu.make_async_copy(a, a_hbm, h_sem.at[tiles])
    a_out.start()
    outs = [gu_out(n) for n in range(len(pieces))] + [pltpu.make_async_copy(dd.at[0], od[0], out_sem.at[len(pieces)])]
    for layer in range(1, layers):
        n = len(outs)
        outs.append(pltpu.make_async_copy(later.at[layer - 1], ogu[layer], out_sem.at[n]))
        outs.append(pltpu.make_async_copy(dd.at[layer], od[layer], out_sem.at[n + 1]))
    down.finish(partner)
    for copy in outs[: len(pieces) + 1]:
        copy.start()
    r = dd.shape[3]
    for n in range(SIDE * SIDE):
        wide_d[r * n : r * (n + 1)] = dd[0, n // SIDE, n % SIDE].astype(F32)
    wd0[...] = wide_d[...].astype(BF)

    def tile_outs(t):
        rows = pl.ds(pl.multiple_of(t * FORWARD_TILE, FORWARD_TILE), FORWARD_TILE)
        return [pltpu.make_async_copy(xv.at[rows], h_hbm.at[rows], h_sem.at[t]), pltpu.make_async_copy(prod.at[rows], prod_hbm.at[rows], p_sem.at[t])]

    def close(t, _):
        for when, step in ((0, "D"), (tiles // 2, "E")):

            @pl.when(t == when)
            def _():
                go(step, *rest)

        rows = pl.ds(pl.multiple_of(t * FORWARD_TILE, FORWARD_TILE), FORWARD_TILE)
        xv[rows] = xv[rows] + dot(prod[rows], wd0[...]).astype(BF)
        for copy in tile_outs(t):
            copy.start()
        return 0

    with jax.named_scope("close"):
        lax.fori_loop(0, tiles, close, 0)
    for unit in rest:
        unit.finish(partner)
    for copy in outs[len(pieces) + 1 :]:
        copy.start()
    for unit in units:
        unit.drain(partner)

    def closed(t, _):
        for copy in tile_outs(t):
            copy.wait()
        return 0

    with jax.named_scope("out_wait"):
        lax.fori_loop(0, tiles, closed, 0)
        for copy in outs + [a_out]:
            copy.wait()


def forward(x, wg, wu, wd):
    tokens, d = x.shape
    layers, rows, ff = wg.shape
    rows_d = wd.shape[1]
    pieces = pieces_of(ff)
    n = 17 * (len(pieces) + 2 * layers - 1)
    anywhere = pl.BlockSpec(memory_space=pl.ANY)
    h, a, prod, *full = pl.pallas_call(
        functools.partial(forward_kernel, layers),
        in_specs=[pl.BlockSpec(memory_space=pltpu.VMEM)] * 3 + [anywhere],
        out_specs=[anywhere] * (3 + 2 * layers),
        out_shape=[jax.ShapeDtypeStruct((tokens, d), BF)] * 2
        + [jax.ShapeDtypeStruct((tokens, ff), BF)]
        + [jax.ShapeDtypeStruct((SIDE, SIDE, rows, 2 * ff), BF)] * layers
        + [jax.ShapeDtypeStruct((SIDE, SIDE, rows_d, d), BF)] * layers,
        scratch_shapes=[pltpu.VMEM((SIDE, SIDE, rows, 2 * (stop - start)), BF) for start, stop in pieces]
        + [
            pltpu.VMEM((layers - 1, SIDE, SIDE, rows, 2 * ff), BF),
            pltpu.VMEM((layers, SIDE, SIDE, rows_d, d), BF),
            pltpu.VMEM((tokens, d), BF),
            pltpu.VMEM((tokens, d), BF),
            pltpu.VMEM((tokens, ff), BF),
            pltpu.VMEM((ff, d), F32),
            pltpu.VMEM((ff, d), BF),
            pltpu.SemaphoreType.DMA((n,)),
            pltpu.SemaphoreType.DMA((n,)),
            pltpu.SemaphoreType.DMA((len(pieces) + 2 * layers - 1,)),
            pltpu.SemaphoreType.DMA((tokens // FORWARD_TILE + 1,)),
            pltpu.SemaphoreType.DMA((tokens // FORWARD_TILE,)),
        ],
        compiler_params=pltpu.CompilerParams(collective_id=1, has_side_effects=True, vmem_limit_bytes=60 * 2**20),
    )(wg, wu, wd, x)
    return h, a, prod, [one.reshape(d, 2 * ff) for one in full[:layers]], [one.reshape(ff, d) for one in full[layers:]]


def hidden_back(both, by):
    g, u, b = both[:, :LANE], both[:, LANE:], by.astype(BF).astype(F32)
    s = jax.nn.sigmoid(g)
    silu = g * s
    return (b * u * (s + silu * (1 - s))).astype(BF), (b * silu).astype(BF), (silu * u).astype(BF)


def layer_kernel(h_ref, dy_ref, wgu_ref, wd_ref, dh_ref, dwgu_ref, dwd_ref, accgu, accd, dgu, prod):
    step, steps = pl.program_id(0), pl.num_programs(0)
    ff = wd_ref.shape[0]

    @pl.when(step == 0)
    def _():
        accgu[...] = jnp.zeros_like(accgu)
        accd[...] = jnp.zeros_like(accd)

    wide = h_ref[...].astype(F32)
    scale = inverse_rms(wide)
    a = (wide * scale).astype(BF)
    dy = dy_ref[...]
    for j in range(0, ff, 2 * LANE):
        c = min(2 * LANE, ff - j)
        both = dot(a, wgu_ref[:, 2 * j : 2 * (j + c)])
        by = dot(dy, wd_ref[j : j + c, :], 1, 1)
        for k in range(0, c, LANE):
            at = j + k
            dg, du, product = hidden_back(both[:, 2 * k : 2 * (k + LANE)], by[:, k : k + LANE])
            prod[:, at : at + LANE] = product
            dgu[:, 2 * at : 2 * at + LANE] = dg
            dgu[:, 2 * at + LANE : 2 * at + 2 * LANE] = du
    da = dot(dgu[...], wgu_ref[...], 1, 1)
    back = scale * (da - wide * (scale * scale * jnp.mean(da * wide, -1, keepdims=True)))
    dh_ref[...] = dy + back.astype(BF)
    accgu[...] += dot(a, dgu[...], 0, 0)
    accd[...] += dot(prod[...], dy, 0, 0)

    @pl.when(step == steps - 1)
    def _():
        r, q = dwgu_ref.shape[2], dwd_ref.shape[2]
        for d in range(SIDE * SIDE):
            dwgu_ref[d // SIDE, d % SIDE] = accgu[r * d : r * (d + 1)].astype(BF)
            dwd_ref[d // SIDE, d % SIDE] = accd[q * d : q * (d + 1)].astype(BF)


def layer_back(h, dy, wgu, wd):
    tokens, d = h.shape
    ff = wd.shape[0]
    n = SIDE * SIDE
    tile = pl.BlockSpec((TILE, d), lambda i: (i, 0))
    whole = lambda shape: pl.BlockSpec(shape, lambda i: (0,) * len(shape))
    gu, dd = (SIDE, SIDE, d // n, 2 * ff), (SIDE, SIDE, ff // n, d)
    return pl.pallas_call(
        layer_kernel,
        grid=(tokens // TILE,),
        in_specs=[tile, tile, whole(wgu.shape), whole(wd.shape)],
        out_specs=[tile, whole(gu), whole(dd)],
        out_shape=[jax.ShapeDtypeStruct((tokens, d), BF), jax.ShapeDtypeStruct(gu, BF), jax.ShapeDtypeStruct(dd, BF)],
        scratch_shapes=[
            pltpu.VMEM((d, 2 * ff), F32),
            pltpu.VMEM((ff, d), F32),
            pltpu.VMEM((TILE, 2 * ff), BF),
            pltpu.VMEM((TILE, ff), BF),
        ],
        compiler_params=pltpu.CompilerParams(vmem_limit_bytes=60 * 2**20),
    )(h, dy, wgu, wd)


class Scatter:
    def __init__(self, terms, bufs, send, recv, base):
        self.terms, self.send, self.recv, self.base = terms, send, recv, base
        self.a, self.b, self.sums, self.out, self.c, self.d = bufs
        self.half = terms.shape[-1] // 2
        r = terms.shape[2]
        if r % 32 == 0:
            self.parts = [(pl.ds(0, r // 2), slice(None)), (pl.ds(r // 2, r // 2), slice(None))]
        else:
            q = self.half // 2
            self.parts = [(slice(None), pl.ds(0, q)), (slice(None), pl.ds(q, q))]

    @staticmethod
    def scratch(rows, columns):
        half = columns // 2
        return [
            pltpu.VMEM((2, 2, SIDE // 2, rows, half), BF),
            pltpu.VMEM((2, 2, SIDE, rows, half), BF),
            pltpu.VMEM((2, SIDE, rows, half), F32),
            pltpu.VMEM((2, SIDE, rows, half), BF),
            pltpu.VMEM((2, rows, half), BF),
            pltpu.VMEM((2, 2, rows, half), BF),
        ]

    def index(self, which, first, second):
        cols = pl.ds(which * self.half, self.half)
        return (second, first, slice(None), cols) if which == 0 else (first, second, slice(None), cols)

    def copies(self, step):
        out = []
        for which, order in enumerate("yx"):
            i1, i2 = ring_places(order)
            for side in range(2):
                by = 1 - 2 * side
                if step == "A":
                    src = self.terms.at[self.index(which, shifted(i1, 2), pl.ds(side * (SIDE // 2), SIDE // 2))]
                    dst = self.a.at[which, side]
                elif step == "B":
                    src = self.terms.at[self.index(which, shifted(i1, by), slice(None))]
                    dst = self.b.at[which, side]
                elif step == "C":
                    rows, cols = self.parts[side]
                    src = self.out.at[which, shifted(i2, 2), rows, cols]
                    dst = self.c.at[which, rows, cols]
                else:
                    src = self.out.at[which, shifted(i2, by)]
                    dst = self.d.at[which, side]
                number = self.base + "ABCD".index(step) * 4 + which * 2 + side
                out.append(
                    pltpu.make_async_remote_copy(
                        src_ref=src,
                        dst_ref=dst,
                        send_sem=self.send.at[number],
                        recv_sem=self.recv.at[number],
                        device_id=along(order, by, step in "CD"),
                        device_id_type=MESH,
                    )
                )
        return out

    def advance(self, step):
        if step != "A":
            with jax.named_scope(f"wait_{step}{self.base // 16}"):
                for copy in self.copies("ABCD"["ABCDE".index(step) - 1]):
                    copy.wait_recv()
        for which, order in enumerate("yx"):
            i1, i2 = ring_places(order)
            if step == "B":
                for side in range(2):
                    for k in range(SIDE // 2):
                        at = self.index(which, shifted(i1, 1 - 2 * side), side * (SIDE // 2) + k)
                        self.terms[at] = (self.terms[at].astype(F32) + self.a[which, side, k].astype(F32)).astype(BF)
            elif step == "C":

                def own(k, _):
                    mine = self.terms[self.index(which, i1, k)].astype(F32)
                    self.sums[which, k] = mine + self.b[which, 0, k].astype(F32) + self.b[which, 1, k].astype(F32)
                    return 0

                lax.fori_loop(0, SIDE, own, 0)
                far = shifted(i2, 2)
                self.out[which, far] = self.sums[which, far].astype(BF)
            elif step == "D":
                for side in range(2):
                    near = shifted(i2, 1 - 2 * side)
                    for part in range(2):
                        at = self.parts[part]
                        value = self.sums[(which, near) + at]
                        if part == side:
                            value = value + self.c[(which,) + at].astype(F32)
                        self.out[(which, near) + at] = value.astype(BF)
        if step != "E":
            for copy in self.copies(step):
                copy.start()

    def result(self):
        halves = []
        for which, order in enumerate("yx"):
            _, i2 = ring_places(order)
            total = self.sums[which, i2] + self.d[which, 0].astype(F32) + self.d[which, 1].astype(F32)
            halves.append(total.astype(BF))
        return halves

    def drain(self):
        for step in "ABCD":
            for copy in self.copies(step):
                copy.wait_send()


class DirectScatter(Scatter):
    def __init__(self, terms, bufs, send, recv, base):
        self.terms, self.send, self.recv, self.base = terms, send, recv, base
        self.b, self.sums, self.out, self.d = bufs
        self.half = terms.shape[-1] // 2

    @staticmethod
    def scratch(rows, columns):
        half = columns // 2
        return [
            pltpu.VMEM((2, len(HOPS), SIDE, rows, half), BF),
            pltpu.VMEM((2, SIDE, rows, half), F32),
            pltpu.VMEM((2, SIDE, rows, half), BF),
            pltpu.VMEM((2, len(HOPS), rows, half), BF),
        ]

    def copies(self, step):
        out = []
        for which, order in enumerate("yx"):
            i1, i2 = ring_places(order)
            for k, by in enumerate(HOPS):
                if step == "A":
                    src, dst = self.terms.at[self.index(which, shifted(i1, by), slice(None))], self.b.at[which, k]
                else:
                    src, dst = self.out.at[which, shifted(i2, by)], self.d.at[which, k]
                number = self.base + (step == "C") * 6 + which * 3 + k
                out.append(
                    pltpu.make_async_remote_copy(
                        src_ref=src,
                        dst_ref=dst,
                        send_sem=self.send.at[number],
                        recv_sem=self.recv.at[number],
                        device_id=along(order, by, step == "C"),
                        device_id_type=MESH,
                    )
                )
        return out

    def advance(self, step):
        if step != "A":
            with jax.named_scope(f"wait_{step}{self.base // 16}"):
                for copy in self.copies("A" if step == "C" else "C"):
                    copy.wait_recv()
        if step == "C":
            for which, order in enumerate("yx"):
                i1, _ = ring_places(order)
                for k in range(SIDE):
                    total = self.terms[self.index(which, i1, k)].astype(F32)
                    for n in range(len(HOPS)):
                        total += self.b[which, n, k].astype(F32)
                    self.sums[which, k] = total
                    self.out[which, k] = total.astype(BF)
        if step != "E":
            for copy in self.copies(step):
                copy.start()

    def result(self):
        halves = []
        for which, order in enumerate("yx"):
            _, i2 = ring_places(order)
            total = self.sums[which, i2]
            for n in range(len(HOPS)):
                total += self.d[which, n].astype(F32)
            halves.append(total.astype(BF))
        return halves

    def drain(self):
        for step in "AC":
            for copy in self.copies(step):
                copy.wait_send()


def sum_everywhere(value, mine, theirs, send, recv, base):
    for which, order in enumerate("yx"):
        mine[which] = jnp.broadcast_to(value, mine.shape[1:])
        copies = [
            pltpu.make_async_remote_copy(
                src_ref=mine.at[which],
                dst_ref=theirs.at[which, by - 1],
                send_sem=send.at[base + which * 3 + by - 1],
                recv_sem=recv.at[base + which * 3 + by - 1],
                device_id=along(order, by),
                device_id_type=MESH,
            )
            for by in range(1, SIDE)
        ]
        with jax.named_scope(f"squares_{order}"):
            for copy in copies:
                copy.start()
            for copy in copies:
                copy.wait()
        value = value + theirs[which, 0][:1, :1] + theirs[which, 1][:1, :1] + theirs[which, 2][:1, :1]
    return value


def chunks_of(ff):
    cuts = [0, 4 * LANE, 8 * LANE, ff - LANE, ff]
    return list(zip(cuts[:-1], cuts[1:]))


def kinds_of(units):
    return [Scatter] * (units - 2) + [DirectScatter] * 2


def back_kernel(chunks, a_hbm, dh_hbm, wgu_hbm, wd_hbm, prod_hbm, gu_hbm, dd_hbm, rg, ru, rd, total, *refs):
    n_units = 3 + len(chunks)
    terms, refs = refs[:n_units], refs[n_units:]
    units = []
    for n, kind in enumerate(kinds_of(n_units)):
        count = len(kind.scratch(1, 2))
        units.append((kind, terms[n], refs[:count], 16 * n))
        refs = refs[count:]
    a, dh, wgu, wd, pbuf, accd, accg, dgu, mine, theirs, send, recv, load, p_sem = refs
    tokens, d = a.shape
    tiles = tokens // BACK_TILE
    units = [kind(term, bufs, send, recv, base) for kind, term, bufs, base in units]
    gu1, dd1, dd0, *parts = units
    pairs = [(gu_hbm, terms[0]), (dd_hbm, terms[1]), (dh_hbm, dh), (a_hbm, a), (wgu_hbm, wgu), (wd_hbm, wd)]
    loads = [pltpu.make_async_copy(source, to, load.at[n]) for n, (source, to) in enumerate(pairs)]
    rows_of = lambda t: pl.ds(pl.multiple_of(t * BACK_TILE, BACK_TILE), BACK_TILE)
    prod_load = lambda t: pltpu.make_async_copy(prod_hbm.at[rows_of(t)], pbuf.at[lax.rem(t, 2)], p_sem.at[lax.rem(t, 2)])
    for copy in loads[:3]:
        copy.start()
    prod_load(0).start()
    entry_barrier(others())
    for copy, unit in zip(loads[:2], units[:2], strict=True):
        copy.wait()
        unit.advance("A")
    loads[2].wait()
    accd[...] = jnp.zeros_like(accd)

    def down(t, _):
        @pl.when(t + 1 < tiles)
        def _():
            prod_load(t + 1).start()

        @pl.when(t == 0)
        def _():
            for copy in loads[3:]:
                copy.start()

        rows = rows_of(t)
        prod_load(t).wait()
        accd[...] += dot(pbuf[lax.rem(t, 2)], dh[rows], 0, 0)
        return 0

    with jax.named_scope("down"):
        lax.fori_loop(0, tiles, down, 0)
    q = terms[2].shape[2]
    for n in range(SIDE * SIDE):
        terms[2][n // SIDE, n % SIDE] = accd[q * n : q * (n + 1)].astype(BF)
    gu1.advance("B")
    for copy in loads[3:]:
        copy.wait()
    one, two, three, four = parts
    slots = [
        {4: [(dd1, "B"), (dd0, "A")], 6: [(gu1, "C")]},
        {0: [(one, "A"), (gu1, "D")], 2: [(dd1, "C"), (dd0, "B")], 4: [(one, "B")], 6: [(dd1, "D"), (dd0, "C")]},
        {0: [(two, "A")], 2: [(dd0, "D"), (one, "C")], 4: [(two, "B")], 6: [(one, "D")]},
        {0: [(three, "A")], 4: [(two, "C")]},
    ]
    for (start, stop), term, slot in zip(chunks, terms[3:], slots, strict=True):
        width = 2 * (stop - start)
        accg[:, :width] = jnp.zeros((d, width), F32)

        def chunk(t, _):
            for when, actions in slot.items():

                @pl.when(t == when * tiles // 8)
                def _():
                    for unit, step in actions:
                        unit.advance(step)

            rows = rows_of(t)
            at, by = a[rows], dh[rows]
            for j in range(start, stop, 2 * LANE):
                c = min(2 * LANE, stop - j)
                both = dot(at, wgu[:, 2 * j : 2 * (j + c)])
                back = dot(by, wd[j : j + c, :], 1, 1)
                for k in range(0, c, LANE):
                    dg, du, _ = hidden_back(both[:, 2 * k : 2 * (k + LANE)], back[:, k : k + LANE])
                    to = 2 * (j - start + k)
                    dgu[:, to : to + LANE] = dg
                    dgu[:, to + LANE : to + 2 * LANE] = du
            accg[:, :width] += dot(at, dgu[:, :width], 0, 0)
            return 0

        with jax.named_scope(f"chunk_{start}"):
            lax.fori_loop(0, tiles, chunk, 0)
        r = term.shape[2]
        for n in range(SIDE * SIDE):
            term[n // SIDE, n % SIDE] = accg[r * n : r * (n + 1), :width].astype(BF)
    four.advance("A")
    squares = jnp.zeros((1, 1), F32)

    def taken(unit, layer, start):
        unit.advance("E")
        found = jnp.zeros((1, 1), F32)
        for which, half in enumerate(unit.result()):
            wide = half.astype(F32)
            found += jnp.sum(wide * wide, keepdims=True)
            width = half.shape[1]
            if start is None:
                rd[layer, :, which * width : (which + 1) * width] = half
            else:
                for k in range(0, width, LANE):
                    block = (2 * start + which * width + k) // LANE
                    out = (rg, ru)[block % 2]
                    out[layer, :, block // 2 * LANE : (block // 2 + 1) * LANE] = half[:, k : k + LANE]
        return found

    starts = [start for start, _ in chunks]
    three.advance("C")
    two.advance("D")
    squares += taken(gu1, 1, 0) + taken(dd1, 1, None)
    four.advance("C")
    squares += taken(dd0, 0, None) + taken(one, 0, starts[0])
    squares += taken(two, 0, starts[1]) + taken(three, 0, starts[2])
    squares += taken(four, 0, starts[3])
    total[...] = jnp.broadcast_to(sum_everywhere(squares, mine, theirs, send, recv, 16 * n_units), total.shape)
    for unit in units:
        unit.drain()


def back_and_reduced(a, dh, wgu, wd, prod, gu, dd):
    tokens, d = a.shape
    ff = wd.shape[0]
    rows, rows_d = gu.shape[2], dd.shape[2]
    chunks = chunks_of(ff)
    shapes = [gu.shape, dd.shape, dd.shape] + [gu.shape[:3] + (2 * (stop - start),) for start, stop in chunks]
    widest = 2 * max(stop - start for start, stop in chunks)
    scratch = [pltpu.VMEM(shape, BF) for shape in shapes]
    for shape, kind in zip(shapes, kinds_of(len(shapes)), strict=True):
        scratch += kind.scratch(shape[2], shape[3])
    n = 16 * len(shapes) + 6
    return pl.pallas_call(
        functools.partial(back_kernel, chunks),
        in_specs=[pl.BlockSpec(memory_space=pl.ANY)] * 7,
        out_specs=[pl.BlockSpec(memory_space=pltpu.VMEM)] * 4,
        out_shape=[
            jax.ShapeDtypeStruct((2, rows, ff), BF),
            jax.ShapeDtypeStruct((2, rows, ff), BF),
            jax.ShapeDtypeStruct((2, rows_d, d), BF),
            jax.ShapeDtypeStruct((8, LANE), F32),
        ],
        scratch_shapes=scratch
        + [
            pltpu.VMEM((tokens, d), BF),
            pltpu.VMEM((tokens, d), BF),
            pltpu.VMEM((d, 2 * ff), BF),
            pltpu.VMEM((ff, d), BF),
            pltpu.VMEM((2, BACK_TILE, ff), BF),
            pltpu.VMEM((ff, d), F32),
            pltpu.VMEM((d, widest), F32),
            pltpu.VMEM((BACK_TILE, widest), BF),
            pltpu.VMEM((2, 8, LANE), F32),
            pltpu.VMEM((2, SIDE - 1, 8, LANE), F32),
            pltpu.SemaphoreType.DMA((n,)),
            pltpu.SemaphoreType.DMA((n,)),
            pltpu.SemaphoreType.DMA((6,)),
            pltpu.SemaphoreType.DMA((2,)),
        ],
        compiler_params=pltpu.CompilerParams(collective_id=2, has_side_effects=True, vmem_limit_bytes=62 * 2**20),
    )(a, dh, wgu, wd, prod, gu, dd)


def adamw(w, m, v, g):
    m = 0.9 * m + 0.1 * g
    v = 0.95 * v + 0.05 * g * g
    step = m * lax.rsqrt(v + 1e-8) + 0.1 * w
    return (w - 0.02 * step).astype(jnp.bfloat16), m, v


def solution(mesh):
    group = mesh.shape["dp"]

    def step(x, dy, *arrays):
        weights, m, v = (arrays[i : i + 3] for i in (0, 3, 6))
        h0, by1 = x[0], dy[0]
        h1, a0, prod, wgu, wd = forward(h0, *weights)
        by0, gu1, dd1 = layer_back(h1, by1, wgu[1], wd[1])
        *gradients, total = back_and_reduced(a0, by0, wgu[0], wd[0], prod, gu1, dd1)
        count = group * sum(g.size for g in gradients)
        factor = jnp.minimum(1.0, 0.5 * lax.rsqrt(total[0, 0] / count + 1e-30))
        new = [adamw(w.astype(F32), m, v, g.astype(F32) * factor) for w, m, v, g in zip(weights, m, v, gradients, strict=True)]
        return tuple(one[which] for which in range(3) for one in new)

    states, cut = P(("rep", "dp"), None, None), P(None, "dp", None)
    return jax.shard_map(
        step,
        mesh=mesh,
        in_specs=(states, states) + (cut,) * 9,
        out_specs=(P("rep", "dp", None),) * 9,
        check_vma=False,
    )
```

time: 230 us -> 197 us (0.86)
  Pallas kernels: 222 us -> 190 us
    pallas_call x4 -> x3, Pallas kernels: 222 us -> 190 us  [the longest x1 77.4 us: back_and_reduced(): pl.pallas_call(functools.partial(back_kernel, chunks), in_specs=[pl.Block...]
where the time goes in v2:
time: 197 us
  Pallas kernels  190 us (96%)
  other arithmetic  4.57 us (2%)
    pallas_call x1, Pallas kernels, back_and_reduced(): pl.pallas_call(functools.partial(back_kernel, chunks), in_specs=[pl.Block...  77.4 us
    pallas_call x1, Pallas kernels, layer_back(): pl.pallas_call(layer_kernel, grid=(tokens // TILE,), in_specs=[tile, tile...  60.2 us
    pallas_call x1, Pallas kernels, forward(): pl.pallas_call(functools.partial(forward_kernel, layers), in_specs=[pl.Bl...  52 us
    convert_element_type x2, other arithmetic, adamw(): return ((w - 0.02 * step).astype(jnp.bfloat16), m, v)  4.57 us

profile of v2, /device:TPU:96, one launch (start us, length us, event | category | flops | bytes accessed | tf_op | source)
XLA Modules:
  0.0 196.8 jit_solution(7063978701000877619)
XLA Ops:
  0.6 52.0 %shard_map.178 = (bf16[4096,512]{1,0:T(8,128)(2,1)}, bf16[4096,512]{1,0:T(8,128)(2,1)}, bf16[4096,1408]{1,0:T(8,128)(2,1)}, bf16[4,4,32,2816]{3,2,1,0:T(8,128)(2...) custom-call(bf16[2,32,1408]{2,1,0:T(8,128)(2,1)} %wg_ref.1, ...), custom_call_target="tpu_custom_call" | custom-call | tf_op jit(solution)/shard_map/pallas_call | solution.py:292
  52.6 60.2 %shard_map.179 = (bf16[4096,512]{1,0:T(8,128)(2,1)}, bf16[4,4,32,2816]{3,2,1,0:T(8,128)(2,1)}, bf16[4,4,88,512]{3,2,1,0:T(8,128)(2,1)}) custom-call(bf16[4096,512]{1,0:T(8,128)(2,1)} %get-tuple-element.24.h_ref, bf16[4096,512]{1,0:T(8,128)(2,1)} %bitcast.7, bf16[512,2816]{1,0:T(8,128)(2,1)} %bitcast.10, bf16[1408,512]{1,0:T(8,128)(2,1)} %bitcast.11), custom_call_target="tpu_custom_call" | custom-call | tf_op jit(solution)/shard_map/pallas_call | solution.py:371
  112.8 0.0 copy-start.2
  112.8 0.0 copy-start.3
  112.8 0.0 copy-start.4
  112.8 0.0 copy-start
  112.8 0.0 copy-start.1
  112.8 0.0 copy-start.5
  112.8 0.0 copy-start.6
  112.9 77.4 %shard_map.180 = (bf16[2,32,1408]{2,1,0:T(8,128)(2,1)}, bf16[2,32,1408]{2,1,0:T(8,128)(2,1)}, bf16[2,88,512]{2,1,0:T(8,128)(2,1)}, f32[8,128]{1,0:T(8,128)}) custom-call(bf16[4096,512]{1,0:T(8,128)(2,1)} %get-tuple-element.23.a_hbm, bf16[4096,512]{1,0:T(8,128)(2,1)} %get-tuple-element.27.dh_hbm, bf16[512,2816]{1,0:T(8,128)(2,1)} %bitcast.9, ...), custom_call_target="tpu_custom_call" | custom-call | tf_op jit(solution)/shard_map/pallas_call | solution.py:731
  190.3 1.2 slice.3
  192.2 0.0 copy-done.2
  192.2 0.0 copy-done.3
  192.2 0.0 copy-done.4
  192.2 1.9 fusion.8
  194.1 0.0 copy-done
  194.1 0.0 copy-done.1
  194.1 0.0 copy-done.5
  194.1 0.0 copy-done.6
  194.2 2.6 %fusion.2 = (bf16[2,32,1408]{2,1,0:T(8,128)(2,1)}, f32[2,32,1408]{2,1,0:T(8,128)}, f32[2,32,1408]{2,1,0:T(8,128)}, bf16[2,32,1408]{2,1,0:T(8,128)(2,1)}, f32[2,32,1408]{2,1,0:T(8,128)}, /*index=5*/f32[2,32,1408]{2,1,0:T(8,128)}) fusion(bf16[2,32,1408]{2,1,0:T(8,128)(2,1)S(1)} %copy-done, f32[]{:T(128)} %bitcast.6, ...), kind=kLoop, calls=%fused_computation.11 | loop fusion | flops 3063808 | bytes 3964932 | tf_op jit(solution)/shard_map/convert_element_type | solution.py:766
Async XLA Ops:
  112.8 79.4 %copy-start.2 = (bf16[2,88,512]{2,1,0:T(8,128)(2,1)S(1)}, bf16[2,88,512]{2,1,0:T(8,128)(2,1)}, u32[]{:S(2)}) copy-start(bf16[2,88,512]{2,1,0:T(8,128)(2,1)} %wd_ref.1) | copy-start | bytes 540676
  112.8 79.4 %copy-start.3 = (f32[2,88,512]{2,1,0:T(8,128)S(1)}, f32[2,88,512]{2,1,0:T(8,128)}, u32[]{:S(2)}) copy-start(f32[2,88,512]{2,1,0:T(8,128)} %param.21) | copy-start | bytes 1081348
  112.8 79.4 %copy-start.4 = (f32[2,88,512]{2,1,0:T(8,128)S(1)}, f32[2,88,512]{2,1,0:T(8,128)}, u32[]{:S(2)}) copy-start(f32[2,88,512]{2,1,0:T(8,128)} %param.18) | copy-start | bytes 1081348
  112.8 81.3 %copy-start = (bf16[2,32,1408]{2,1,0:T(8,128)(2,1)S(1)}, bf16[2,32,1408]{2,1,0:T(8,128)(2,1)}, u32[]{:S(2)}) copy-start(bf16[2,32,1408]{2,1,0:T(8,128)(2,1)} %wg_ref.1) | copy-start | bytes 540676
  112.8 81.3 %copy-start.1 = (bf16[2,32,1408]{2,1,0:T(8,128)(2,1)S(1)}, bf16[2,32,1408]{2,1,0:T(8,128)(2,1)}, u32[]{:S(2)}) copy-start(bf16[2,32,1408]{2,1,0:T(8,128)(2,1)} %wu_ref.1) | copy-start | bytes 540676
  112.8 81.3 %copy-start.5 = (f32[2,32,1408]{2,1,0:T(8,128)S(1)}, f32[2,32,1408]{2,1,0:T(8,128)}, u32[]{:S(2)}) copy-start(f32[2,32,1408]{2,1,0:T(8,128)} %param.19) | copy-start | bytes 1081348
  112.8 81.3 %copy-start.6 = (f32[2,32,1408]{2,1,0:T(8,128)S(1)}, f32[2,32,1408]{2,1,0:T(8,128)}, u32[]{:S(2)}) copy-start(f32[2,32,1408]{2,1,0:T(8,128)} %param.16) | copy-start | bytes 1081348

commit v3 on v2

--- a/solution.py
+++ b/solution.py
@@ -59,8 +59,8 @@
 
 
 class Gather:
-    def __init__(self, buf, core, cut, rows, send, recv, base, direct=False):
-        self.steps = "ACE" if direct else "ABCDE"
+    def __init__(self, buf, core, cut, rows, send, recv, base, steps):
+        self.steps = steps
         self.buf, self.core, self.send, self.recv, self.base = buf, core, send, recv, base
         half = buf.shape[-1] // 2
         self.half, self.rows, self.r = half, rows, buf.shape[-2]
@@ -72,11 +72,15 @@
         a, b = (second, first) if order == "y" else (first, second)
         return self.buf.at[a, b, rows, cols]
 
+    def hops(self, step):
+        straight = (step == "A" and "B" not in self.steps) or (step == "C" and "D" not in self.steps)
+        return HOPS if straight else HOPS[:2]
+
     def copies(self, step):
         out = []
         for which, order in enumerate("yx"):
             i1, i2 = ring_places(order)
-            hops = HOPS if self.steps == "ACE" else HOPS[:2]
+            hops = self.hops(step)
             if step == "A":
                 refs = [self.at(order, i1, i2)] * len(hops)
             elif step == "B":
@@ -92,7 +96,8 @@
                     self.at(order, pl.ds(SIDE // 2, SIDE // 2), shifted(i2, 1)),
                 ]
             for side, ref in enumerate(refs):
-                number = self.base + self.steps.index(step) * 2 * len(hops) + which * len(hops) + side
+                before = sum(2 * len(self.hops(one)) for one in self.steps[: self.steps.index(step)])
+                number = self.base + before + which * len(hops) + side
                 out.append(
                     pltpu.make_async_remote_copy(
                         src_ref=ref,
@@ -170,8 +175,9 @@
     entry_barrier(others() + [partner])
 
     def unit_of(n, buf):
+        steps = "ACE" if n == 0 else "ACDE" if n <= len(pieces) else "ABCDE"
         quarter = (buf.shape[-1] // 4 + LANE - 1) // LANE * LANE
-        return Gather(buf, core, quarter, 16 if buf.shape[2] % 32 == 0 else 48, send, recv, 17 * n, n == 0)
+        return Gather(buf, core, quarter, 16 if buf.shape[2] % 32 == 0 else 48, send, recv, 17 * n, steps)
 
     units = [unit_of(n, buf) for n, buf in enumerate(bufs)]
     gus, down, rest = units[: len(pieces)], units[len(pieces)], units[len(pieces) + 1 :]
@@ -192,13 +198,11 @@
 
     with jax.named_scope("norm"):
         lax.fori_loop(0, tiles, norm, 0)
-    go("C", one)
-    go("B", two, three, down)
-    go("C", two)
+    go("C", one, two, three, down)
     go("E", one)
     slots = [
-        {2: [("D", [two]), ("C", [three])], 4: [("C", [down])], 6: [("E", [two]), ("D", [three]), ("A", rest)]},
-        {0: [("D", [down])], 2: [("E", [three]), ("B", rest)], 4: [("E", [down]), ("C", rest)]},
+        {0: [("D", [two])], 2: [("D", [three])], 4: [("D", [down]), ("A", rest)], 6: [("E", [two])]},
+        {0: [("E", [three]), ("B", rest)], 2: [("E", [down])], 4: [("C", rest)]},
         {},
     ]
     for unit, buf, (start, stop), slot in zip(gus, first, pieces, slots, strict=True):
@@ -649,13 +653,15 @@
         copy.wait()
     one, two, three, four = parts
     slots = [
-        {4: [(dd1, "B"), (dd0, "A")], 6: [(gu1, "C")]},
-        {0: [(one, "A"), (gu1, "D")], 2: [(dd1, "C"), (dd0, "B")], 4: [(one, "B")], 6: [(dd1, "D"), (dd0, "C")]},
-        {0: [(two, "A")], 2: [(dd0, "D"), (one, "C")], 4: [(two, "B")], 6: [(one, "D")]},
+        {4: [(dd1, "B"), (dd0, "A")]},
+        {0: [(gu1, "C"), (one, "A")], 2: [(dd1, "C"), (dd0, "B")], 4: [(gu1, "D"), (one, "B")], 6: [(dd1, "D"), (dd0, "C")]},
+        {0: [(two, "A")], 2: [(one, "C"), (dd0, "D")], 4: [(two, "B")], 6: [(one, "D")]},
         {0: [(three, "A")], 4: [(two, "C")]},
     ]
     for (start, stop), term, slot in zip(chunks, terms[3:], slots, strict=True):
         width = 2 * (stop - start)
+        tile = BACK_TILE if stop < chunks[-1][1] else 2 * BACK_TILE
+        tiles = tokens // tile
         accg[:, :width] = jnp.zeros((d, width), F32)
 
         def chunk(t, _):
@@ -666,8 +672,9 @@
                     for unit, step in actions:
                         unit.advance(step)
 
-            rows = rows_of(t)
+            rows = pl.ds(pl.multiple_of(t * tile, tile), tile)
             at, by = a[rows], dh[rows]
+            to_rows = pl.ds(0, tile)
             for j in range(start, stop, 2 * LANE):
                 c = min(2 * LANE, stop - j)
                 both = dot(at, wgu[:, 2 * j : 2 * (j + c)])
@@ -675,9 +682,9 @@
                 for k in range(0, c, LANE):
                     dg, du, _ = hidden_back(both[:, 2 * k : 2 * (k + LANE)], back[:, k : k + LANE])
                     to = 2 * (j - start + k)
-                    dgu[:, to : to + LANE] = dg
-                    dgu[:, to + LANE : to + 2 * LANE] = du
-            accg[:, :width] += dot(at, dgu[:, :width], 0, 0)
+                    dgu[to_rows, to : to + LANE] = dg
+                    dgu[to_rows, to + LANE : to + 2 * LANE] = du
+            accg[:, :width] += dot(at, dgu[to_rows, :width], 0, 0)
             return 0
 
         with jax.named_scope(f"chunk_{start}"):
@@ -747,7 +754,7 @@
             pltpu.VMEM((2, BACK_TILE, ff), BF),
             pltpu.VMEM((ff, d), F32),
             pltpu.VMEM((d, widest), F32),
-            pltpu.VMEM((BACK_TILE, widest), BF),
+            pltpu.VMEM((2 * BACK_TILE, widest), BF),
             pltpu.VMEM((2, 8, LANE), F32),
             pltpu.VMEM((2, SIDE - 1, 8, LANE), F32),
             pltpu.SemaphoreType.DMA((n,)),
@@ -766,6 +773,28 @@
     return (w - 0.02 * step).astype(jnp.bfloat16), m, v
 
 
+def update_kernel(count, total_ref, *refs):
+    inputs, outputs = refs[:12], refs[12:]
+    factor = jnp.minimum(1.0, 0.5 * lax.rsqrt(total_ref[:1, :1] / count + 1e-30))
+    for i in range(3):
+        w, m, v, g = inputs[i::3]
+        for layer in range(w.shape[0]):
+            new = adamw(w[layer].astype(F32), m[layer], v[layer], g[layer].astype(F32) * factor)
+            for to, value in zip(outputs[i::3], new, strict=True):
+                to[layer] = value
+
+
+def updated(count, total, weights, m, v, gradients):
+    inputs = [*weights, *m, *v, *gradients]
+    return pl.pallas_call(
+        functools.partial(update_kernel, count),
+        in_specs=[pl.BlockSpec(memory_space=pltpu.VMEM)] * 13,
+        out_specs=[pl.BlockSpec(memory_space=pltpu.VMEM)] * 9,
+        out_shape=[jax.ShapeDtypeStruct(one.shape, one.dtype) for one in inputs[:9]],
+        compiler_params=pltpu.CompilerParams(vmem_limit_bytes=62 * 2**20),
+    )(total, *inputs)
+
+
 def solution(mesh):
     group = mesh.shape["dp"]
 
@@ -776,9 +805,7 @@
         by0, gu1, dd1 = layer_back(h1, by1, wgu[1], wd[1])
         *gradients, total = back_and_reduced(a0, by0, wgu[0], wd[0], prod, gu1, dd1)
         count = group * sum(g.size for g in gradients)
-        factor = jnp.minimum(1.0, 0.5 * lax.rsqrt(total[0, 0] / count + 1e-30))
-        new = [adamw(w.astype(F32), m, v, g.astype(F32) * factor) for w, m, v, g in zip(weights, m, v, gradients, strict=True)]
-        return tuple(one[which] for which in range(3) for one in new)
+        return tuple(updated(count, total, weights, m, v, gradients))
 
     states, cut = P(("rep", "dp"), None, None), P(None, "dp", None)
     return jax.shard_map(

time: 197 us -> 187 us (0.949)
  other arithmetic: 4.57 us -> 0 us
  Pallas kernels: 190 us -> 186 us
    pallas_call x1, Pallas kernels: 77.4 us -> 72.7 us  [back_and_reduced(): pl.pallas_call(functools.partial(back_kernel, chunks), in_specs=[pl.Block...]
    convert_element_type x2 -> x0, other arithmetic: 4.57 us -> none  [adamw(): return ((w - 0.02 * step).astype(jnp.bfloat16), m, v)]
    pallas_call x0 -> x1, Pallas kernels: none -> 3.79 us  [updated(): pl.pallas_call(functools.partial(update_kernel, count), in_specs=[pl.Bloc...]
    pallas_call x1, Pallas kernels: 52 us -> 49.6 us  [forward(): pl.pallas_call(functools.partial(forward_kernel, layers), in_specs=[pl.Bl...]
where the time goes in v3:
time: 187 us
  Pallas kernels  186 us (99%)
    pallas_call x1, Pallas kernels, back_and_reduced(): pl.pallas_call(functools.partial(back_kernel, chunks), in_specs=[pl.Block...  72.7 us
    pallas_call x1, Pallas kernels, layer_back(): pl.pallas_call(layer_kernel, grid=(tokens // TILE,), in_specs=[tile, tile...  60.1 us
    pallas_call x1, Pallas kernels, forward(): pl.pallas_call(functools.partial(forward_kernel, layers), in_specs=[pl.Bl...  49.6 us
    pallas_call x1, Pallas kernels, updated(): pl.pallas_call(functools.partial(update_kernel, count), in_specs=[pl.Bloc...  3.79 us

profile of v3, /device:TPU:96, one launch (start us, length us, event | category | flops | bytes accessed | tf_op | source)
XLA Modules:
  0.0 187.0 jit_solution(18014594455729632410)
XLA Ops:
  0.6 49.6 %shard_map.178 = (bf16[4096,512]{1,0:T(8,128)(2,1)}, bf16[4096,512]{1,0:T(8,128)(2,1)}, bf16[4096,1408]{1,0:T(8,128)(2,1)}, bf16[4,4,32,2816]{3,2,1,0:T(8,128)(2...) custom-call(bf16[2,32,1408]{2,1,0:T(8,128)(2,1)} %refs_0_.1, ...), custom_call_target="tpu_custom_call" | custom-call | tf_op jit(solution)/shard_map/pallas_call | solution.py:296
  50.2 60.1 %shard_map.179 = (bf16[4096,512]{1,0:T(8,128)(2,1)}, bf16[4,4,32,2816]{3,2,1,0:T(8,128)(2,1)}, bf16[4,4,88,512]{3,2,1,0:T(8,128)(2,1)}) custom-call(bf16[4096,512]{1,0:T(8,128)(2,1)} %get-tuple-element.24.h_ref, bf16[4096,512]{1,0:T(8,128)(2,1)} %bitcast.6, bf16[512,2816]{1,0:T(8,128)(2,1)} %bitcast.9, bf16[1408,512]{1,0:T(8,128)(2,1)} %bitcast.10), custom_call_target="tpu_custom_call" | custom-call | tf_op jit(solution)/shard_map/pallas_call | solution.py:375
  110.4 72.7 %shard_map.180 = (bf16[2,32,1408]{2,1,0:T(8,128)(2,1)}, bf16[2,32,1408]{2,1,0:T(8,128)(2,1)}, bf16[2,88,512]{2,1,0:T(8,128)(2,1)}, f32[8,128]{1,0:T(8,128)}) custom-call(bf16[4096,512]{1,0:T(8,128)(2,1)} %get-tuple-element.23.a_hbm, bf16[4096,512]{1,0:T(8,128)(2,1)} %get-tuple-element.27.dh_hbm, bf16[512,2816]{1,0:T(8,128)(2,1)} %bitcast.8, ...), custom_call_target="tpu_custom_call" | custom-call | tf_op jit(solution)/shard_map/pallas_call | solution.py:738
  183.0 3.8 %shard_map.181 = (bf16[2,32,1408]{2,1,0:T(8,128)(2,1)}, bf16[2,32,1408]{2,1,0:T(8,128)(2,1)}, bf16[2,88,512]{2,1,0:T(8,128)(2,1)}, f32[2,32,1408]{2,1,0:T(8,128)...) custom-call(f32[8,128]{1,0:T(8,128)} %get-tuple-element.33.total_ref, ...), custom_call_target="tpu_custom_call" | custom-call | tf_op jit(solution)/shard_map/pallas_call | solution.py:789

commit v4 on v3

--- a/solution.py
+++ b/solution.py
@@ -238,9 +238,11 @@
     a_out.start()
     outs = [gu_out(n) for n in range(len(pieces))] + [pltpu.make_async_copy(dd.at[0], od[0], out_sem.at[len(pieces)])]
     for layer in range(1, layers):
-        n = len(outs)
-        outs.append(pltpu.make_async_copy(later.at[layer - 1], ogu[layer], out_sem.at[n]))
-        outs.append(pltpu.make_async_copy(dd.at[layer], od[layer], out_sem.at[n + 1]))
+        for source, to in ((later.at[layer - 1], ogu[layer]), (dd.at[layer], od[layer])):
+            half = source.shape[-1] // 2
+            for owner in (core, 1 - core):
+                cols = pl.ds(pl.multiple_of(owner * half, LANE), half)
+                outs.append(pltpu.make_async_copy(source.at[:, :, :, cols], to.at[:, :, :, cols], out_sem.at[len(outs)]))
     down.finish(partner)
     for copy in outs[: len(pieces) + 1]:
         copy.start()
@@ -259,6 +261,9 @@
             @pl.when(t == when)
             def _():
                 go(step, *rest)
+                if step == "E":
+                    for copy in outs[len(pieces) + 1 :: 2]:
+                        copy.start()
 
         rows = pl.ds(pl.multiple_of(t * FORWARD_TILE, FORWARD_TILE), FORWARD_TILE)
         xv[rows] = xv[rows] + dot(prod[rows], wd0[...]).astype(BF)
@@ -270,7 +275,7 @@
         lax.fori_loop(0, tiles, close, 0)
     for unit in rest:
         unit.finish(partner)
-    for copy in outs[len(pieces) + 1 :]:
+    for copy in outs[len(pieces) + 2 :: 2]:
         copy.start()
     for unit in units:
         unit.drain(partner)
@@ -312,7 +317,7 @@
             pltpu.VMEM((ff, d), BF),
             pltpu.SemaphoreType.DMA((n,)),
             pltpu.SemaphoreType.DMA((n,)),
-            pltpu.SemaphoreType.DMA((len(pieces) + 2 * layers - 1,)),
+            pltpu.SemaphoreType.DMA((len(pieces) + 4 * layers - 3,)),
             pltpu.SemaphoreType.DMA((tokens // FORWARD_TILE + 1,)),
             pltpu.SemaphoreType.DMA((tokens // FORWARD_TILE,)),
         ],
@@ -569,7 +574,7 @@
                 copy.wait_send()
 
 
-def sum_everywhere(value, mine, theirs, send, recv, base):
+def sum_everywhere(value, mine, theirs, send, recv, base, meanwhile):
     for which, order in enumerate("yx"):
         mine[which] = jnp.broadcast_to(value, mine.shape[1:])
         copies = [
@@ -586,6 +591,8 @@
         with jax.named_scope(f"squares_{order}"):
             for copy in copies:
                 copy.start()
+            if which == 0:
+                meanwhile()
             for copy in copies:
                 copy.wait()
         value = value + theirs[which, 0][:1, :1] + theirs[which, 1][:1, :1] + theirs[which, 2][:1, :1]
@@ -601,7 +608,7 @@
     return [Scatter] * (units - 2) + [DirectScatter] * 2
 
 
-def back_kernel(chunks, a_hbm, dh_hbm, wgu_hbm, wd_hbm, prod_hbm, gu_hbm, dd_hbm, rg, ru, rd, total, *refs):
+def back_kernel(chunks, a_hbm, dh_hbm, wgu_hbm, wd_hbm, prod_hbm, gu_hbm, dd_hbm, rg_hbm, ru_hbm, rd_hbm, total, *refs):
     n_units = 3 + len(chunks)
     terms, refs = refs[:n_units], refs[n_units:]
     units = []
@@ -609,7 +616,7 @@
         count = len(kind.scratch(1, 2))
         units.append((kind, terms[n], refs[:count], 16 * n))
         refs = refs[count:]
-    a, dh, wgu, wd, pbuf, accd, accg, dgu, mine, theirs, send, recv, load, p_sem = refs
+    rg, ru, rd, a, dh, wgu, wd, pbuf, accd, accg, dgu, mine, theirs, send, recv, load, p_sem, out_sem = refs
     tokens, d = a.shape
     tiles = tokens // BACK_TILE
     units = [kind(term, bufs, send, recv, base) for kind, term, bufs, base in units]
@@ -719,9 +726,17 @@
     squares += taken(dd0, 0, None) + taken(one, 0, starts[0])
     squares += taken(two, 0, starts[1]) + taken(three, 0, starts[2])
     squares += taken(four, 0, starts[3])
-    total[...] = jnp.broadcast_to(sum_everywhere(squares, mine, theirs, send, recv, 16 * n_units), total.shape)
-    for unit in units:
-        unit.drain()
+    outs = [pltpu.make_async_copy(source, to, out_sem.at[n]) for n, (source, to) in enumerate(((rg, rg_hbm), (ru, ru_hbm), (rd, rd_hbm)))]
+
+    def meanwhile():
+        for copy in outs:
+            copy.start()
+        for unit in units:
+            unit.drain()
+
+    total[...] = jnp.broadcast_to(sum_everywhere(squares, mine, theirs, send, recv, 16 * n_units, meanwhile), total.shape)
+    for copy in outs:
+        copy.wait()
 
 
 def back_and_reduced(a, dh, wgu, wd, prod, gu, dd):
@@ -738,7 +753,7 @@
     return pl.pallas_call(
         functools.partial(back_kernel, chunks),
         in_specs=[pl.BlockSpec(memory_space=pl.ANY)] * 7,
-        out_specs=[pl.BlockSpec(memory_space=pltpu.VMEM)] * 4,
+        out_specs=[pl.BlockSpec(memory_space=pl.ANY)] * 3 + [pl.BlockSpec(memory_space=pltpu.VMEM)],
         out_shape=[
             jax.ShapeDtypeStruct((2, rows, ff), BF),
             jax.ShapeDtypeStruct((2, rows, ff), BF),
@@ -747,6 +762,9 @@
         ],
         scratch_shapes=scratch
         + [
+            pltpu.VMEM((2, rows, ff), BF),
+            pltpu.VMEM((2, rows, ff), BF),
+            pltpu.VMEM((2, rows_d, d), BF),
             pltpu.VMEM((tokens, d), BF),
             pltpu.VMEM((tokens, d), BF),
             pltpu.VMEM((d, 2 * ff), BF),
@@ -761,6 +779,7 @@
             pltpu.SemaphoreType.DMA((n,)),
             pltpu.SemaphoreType.DMA((6,)),
             pltpu.SemaphoreType.DMA((2,)),
+            pltpu.SemaphoreType.DMA((3,)),
         ],
         compiler_params=pltpu.CompilerParams(collective_id=2, has_side_effects=True, vmem_limit_bytes=62 * 2**20),
     )(a, dh, wgu, wd, prod, gu, dd)

time: 187 us -> 186 us (level)
  no operation moved by 1% of the time
where the time goes in v4:
time: 186 us
  Pallas kernels  185 us (99%)
    pallas_call x1, Pallas kernels, back_and_reduced(): pl.pallas_call(functools.partial(back_kernel, chunks), in_specs=[pl.Block...  72.3 us
    pallas_call x1, Pallas kernels, layer_back(): pl.pallas_call(layer_kernel, grid=(tokens // TILE,), in_specs=[tile, tile...  60.1 us
    pallas_call x1, Pallas kernels, forward(): pl.pallas_call(functools.partial(forward_kernel, layers), in_specs=[pl.Bl...  48.9 us
    pallas_call x1, Pallas kernels, updated(): pl.pallas_call(functools.partial(update_kernel, count), in_specs=[pl.Bloc...  3.79 us

profile of v4, /device:TPU:96, one launch (start us, length us, event | category | flops | bytes accessed | tf_op | source)
XLA Modules:
  0.0 186.0 jit_solution(12869676449918437186)
XLA Ops:
  0.6 48.9 %shard_map.178 = (bf16[4096,512]{1,0:T(8,128)(2,1)}, bf16[4096,512]{1,0:T(8,128)(2,1)}, bf16[4096,1408]{1,0:T(8,128)(2,1)}, bf16[4,4,32,2816]{3,2,1,0:T(8,128)(2...) custom-call(bf16[2,32,1408]{2,1,0:T(8,128)(2,1)} %refs_0_.1, ...), custom_call_target="tpu_custom_call" | custom-call | tf_op jit(solution)/shard_map/pallas_call | solution.py:301
  49.6 60.1 %shard_map.179 = (bf16[4096,512]{1,0:T(8,128)(2,1)}, bf16[4,4,32,2816]{3,2,1,0:T(8,128)(2,1)}, bf16[4,4,88,512]{3,2,1,0:T(8,128)(2,1)}) custom-call(bf16[4096,512]{1,0:T(8,128)(2,1)} %get-tuple-element.24.h_ref, bf16[4096,512]{1,0:T(8,128)(2,1)} %bitcast.6, bf16[512,2816]{1,0:T(8,128)(2,1)} %bitcast.9, bf16[1408,512]{1,0:T(8,128)(2,1)} %bitcast.10), custom_call_target="tpu_custom_call" | custom-call | tf_op jit(solution)/shard_map/pallas_call | solution.py:380
  109.7 72.3 %shard_map.180 = (bf16[2,32,1408]{2,1,0:T(8,128)(2,1)}, bf16[2,32,1408]{2,1,0:T(8,128)(2,1)}, bf16[2,88,512]{2,1,0:T(8,128)(2,1)}, f32[8,128]{1,0:T(8,128)}) custom-call(bf16[4096,512]{1,0:T(8,128)(2,1)} %get-tuple-element.23.a_hbm, bf16[4096,512]{1,0:T(8,128)(2,1)} %get-tuple-element.27.dh_hbm, bf16[512,2816]{1,0:T(8,128)(2,1)} %bitcast.8, ...), custom_call_target="tpu_custom_call" | custom-call | tf_op jit(solution)/shard_map/pallas_call | solution.py:753
  182.0 3.8 %shard_map.181 = (bf16[2,32,1408]{2,1,0:T(8,128)(2,1)}, bf16[2,32,1408]{2,1,0:T(8,128)(2,1)}, bf16[2,88,512]{2,1,0:T(8,128)(2,1)}, f32[2,32,1408]{2,1,0:T(8,128)...) custom-call(f32[8,128]{1,0:T(8,128)} %get-tuple-element.33.total_ref, ...), custom_call_target="tpu_custom_call" | custom-call | tf_op jit(solution)/shard_map/pallas_call | solution.py:808
